TPU v7x, 256 devices: a whole 4x4x8 slice. The times are simulated.
256 devices in a mesh: src: 128 (over z, y, x_lo, core), tgt: 2 (over x_hi).
Axes of the slice: x: 4 (x_hi: 2, x_lo: 2; x = x_hi * 2 + x_lo), y: 4, z: 8, core: 2. Of those that a mesh axis runs over, the one named last changes fastest.
Arguments:
- positions: float32 [3, 32768], P(None, ('src', 'tgt')), may hold values from -1.3 to 1.3, as said below
- areas: float32 [32768], P(('src', 'tgt')), may hold values from 0.25 to 4
- right_side: float32 [3, 32768], P(None, ('src', 'tgt')), may hold values from -6 to 6
Outputs:
- solution_field: float32 [3, 32768], P(None, ('src', 'tgt'))
- residual: float32 [3, 32768], P(None, ('src', 'tgt'))
- hessenberg: float32 [5, 4], replicated
Inputs may be any that keep to these rules, and one draw needn't show every extreme that they name: positions lie on a sphere of radius 1 or an ellipsoid centred at the anchor with semi-axes between 0.7 and 1.3, with no locality in how panels are assigned to devices.
All inputs are finite; a program needn't handle non-finite values.
Results may differ from a plain program's by a relative error of at most 0.0003.
Values sent between devices are 32-bit elements.
A program may use at most 64 MiB of HBM per device.

v0:
```python
import functools
import math

import jax
import jax.numpy as jnp
from jax import lax
from jax.sharding import Mesh
from jax.sharding import PartitionSpec as P

ITERS = 4
SRC = ("src_0", "src_1", "src_2", "src_3")
SRC_TGT = ("src_0", "src_1", "src_2", "src_3", "tgt")


soften = 0.0025
column_block = 2048


def laid_out(parts, dim):
    lengths = list(parts.shape[1:])
    lengths[dim] *= parts.shape[0]
    return jnp.moveaxis(parts, 0, dim).reshape(lengths)


def all_blocks(value, axes, turns):
    parts = value
    for k in turns:
        parts = lax.all_gather(parts, axes[k])
    done = turns[::-1]
    back = [done.index(k) for k in range(len(axes))]
    parts = parts.transpose(*back, *range(len(axes), parts.ndim))
    return parts.reshape(-1, *value.shape)


def gathered_by_axis(value, axes, turns, dim):
    return laid_out(all_blocks(value, axes, turns), dim)


def one_axis_at_a_time(value, axes):
    return functools.reduce(lax.psum, axes, value)


def stokes_block(targets, sources, densities):
    offset = targets[:, :, None] - sources[:, None, :]
    square = jnp.sum(offset * offset, axis=0) + soften
    factor = square ** (-1.5)
    projected = jnp.sum(offset * densities[:, None, :], axis=0)
    return jnp.sum(
        factor[None] * ((square + soften)[None] * densities[:, None, :] + offset * projected[None]),
        axis=2,
    )


def stokes_sum(targets, sources, densities):
    columns = sources.shape[1]
    stride = math.gcd(columns, column_block)
    blocks = columns // stride
    if blocks == 1:
        return stokes_block(targets, sources, densities)
    source_blocks = sources.reshape(3, blocks, stride).transpose(1, 0, 2)
    density_blocks = densities.reshape(3, blocks, stride).transpose(1, 0, 2)

    def accumulate(accumulated, block_pair):
        return (accumulated + stokes_block(targets, block_pair[0], block_pair[1]), None)

    accumulated, unused = lax.scan(
        accumulate, jnp.zeros((3, targets.shape[1]), jnp.float32), (source_blocks, density_blocks)
    )
    return accumulated


def least_squares(hessenberg, initial):
    columns = hessenberg.shape[1]
    triangle = hessenberg
    target = jnp.zeros((hessenberg.shape[0],), jnp.float32).at[0].set(initial)
    for column in range(columns):
        leading = triangle[column, column]
        second = triangle[column + 1, column]
        radius = jnp.sqrt(leading * leading + second * second)
        cosine = leading / radius
        sine_value = second / radius
        row_top = triangle[column]
        row_low = triangle[column + 1]
        triangle = triangle.at[column].set(cosine * row_top + sine_value * row_low)
        triangle = triangle.at[column + 1].set(cosine * row_low - sine_value * row_top)
        target_top = target[column]
        target_low = target[column + 1]
        target = target.at[column].set(cosine * target_top + sine_value * target_low)
        target = target.at[column + 1].set(cosine * target_low - sine_value * target_top)
    solution = jnp.zeros((columns,), jnp.float32)
    for row_index in reversed(range(columns)):
        partial_sum = jnp.sum(
            triangle[row_index, row_index + 1 : columns] * solution[row_index + 1 : columns]
        )
        solution = solution.at[row_index].set(
            (target[row_index] - partial_sum) / triangle[row_index, row_index]
        )
    return solution


def shards(positions, areas, right_side):
    device_count = lax.axis_size(SRC) * lax.axis_size("tgt")
    coefficient = float(positions.shape[1] * device_count) ** (-0.5)
    weights = areas * coefficient
    target_pair = lax.all_gather(positions, "tgt", axis=1, tiled=True)
    own_half = gathered_by_axis(positions, (("src_0", "src_1", "src_2"), "src_3"), (0, 1), 1)

    def apply_operator(vector):
        weighted = vector * weights[None, :]

        def absorb(accumulated, piece):
            sources = lax.slice_in_dim(own_half, 0, piece.shape[1], axis=1)
            return accumulated + stokes_sum(target_pair, sources, piece)

        partial_image = absorb(
            jnp.zeros((3, target_pair.shape[1]), jnp.float32),
            jax.tree.map(
                lambda part: gathered_by_axis(
                    part, (("src_0", "src_1", "src_2"), "src_3"), (0, 1), 1
                ),
                weighted,
            ),
        )
        return vector + lax.psum_scatter(partial_image, "tgt", scatter_dimension=1, tiled=True)

    initial = jnp.sqrt(one_axis_at_a_time(jnp.sum(right_side * right_side), SRC_TGT))
    krylov_basis = [right_side / initial]
    hessenberg = jnp.zeros((ITERS + 1, ITERS), jnp.float32)
    for iteration in range(ITERS):
        applied = apply_operator(krylov_basis[iteration])
        stacked = jnp.stack(krylov_basis)
        projections = one_axis_at_a_time(jnp.sum(stacked * applied[None], axis=(1, 2)), SRC_TGT)
        remainder = applied - jnp.sum(projections[:, None, None] * stacked, axis=0)
        height = jnp.sqrt(one_axis_at_a_time(jnp.sum(remainder * remainder), SRC_TGT))
        hessenberg = hessenberg.at[: iteration + 1, iteration].set(projections)
        hessenberg = hessenberg.at[iteration + 1, iteration].set(height)
        krylov_basis.append(remainder / height)
    coefficients = least_squares(hessenberg, initial)
    stacked = jnp.stack(krylov_basis)
    solution_field = jnp.sum(coefficients[:, None, None] * stacked[:ITERS], axis=0)
    misfit = -jnp.sum(hessenberg * coefficients[None, :], axis=1)
    misfit = misfit.at[0].add(initial)
    residual = jnp.sum(misfit[:, None, None] * stacked, axis=0)
    return (solution_field, residual, hessenberg)


def solution(mesh):
    split = Mesh(
        mesh.devices.reshape(8, 4, 2, 2, mesh.shape["tgt"]),
        ("src_0", "src_1", "src_2", "src_3", "tgt"),
    )
    placed = (P(None, SRC_TGT), P(SRC_TGT), P(None, SRC_TGT))
    return jax.shard_map(
        shards,
        mesh=split,
        in_specs=placed,
        out_specs=(P(None, SRC_TGT), P(None, SRC_TGT), P()),
        check_vma=False,
    )
```

profile of v0, /device:TPU:1, one launch (start us, length us, event | category | flops | bytes accessed | tf_op | source)
XLA Modules:
  0.0 1409.9 jit_solution(11649465368085691450)
XLA Ops:
  8.5 17.9 %psum.315 = f32[]{:T(128)} all-reduce(f32[]{:T(128)} %multiply_reduce_fusion.14), channel_id=1, replica_groups=mesh['src_0'=8,'src_1'=4,'src_2'=2,'src_3'=2,'tgt'=2] {'src_0'}, use_global_device_ids=true, to_apply=%region_1.0 | all-reduce | flops 1 | bytes 8 | tf_op jit(solution)/shard_map/psum | solution.py:40
  58.2 124.3 %all-gather.11 = f32[64,3,128]{2,1,0:T(4,128)S(1)} all-gather(f32[1,3,128]{2,1,0:T(4,128)S(1)} %multiply_bitcast_fusion.3), channel_id=4, replica_groups=mesh['src_0'=8,'src_1'=4,'src_2'=2,'src_3'=2,'tgt'=2] {'src_0','src_1','..., dimensions={0}, use_global_device_ids=true | all-gather | bytes 99840 | tf_op jit(solution)/shard_map/all_gather | solution.py:28
  182.5 30.7 %all-gather.3 = f32[128,3,128]{2,0,1:T(8,128)S(1)} all-gather(f32[64,3,128]{2,0,1:T(8,128)S(1)} %copy.34), channel_id=5, replica_groups=mesh['src_0'=8,'src_1'=4,'src_2'=2,'src_3'=2,'tgt'=2] {'src_3'}, dimensions={0}, use_global_device_ids=true | all-gather | bytes 294912 | tf_op jit(solution)/shard_map/all_gather | solution.py:28
  218.3 123.3 %all-gather.10 = f32[64,3,128]{2,1,0:T(4,128)S(1)} all-gather(f32[1,3,128]{2,1,0:T(4,128)} %bitcast.167), channel_id=2, replica_groups=mesh['src_0'=8,'src_1'=4,'src_2'=2,'src_3'=2,'tgt'=2] {'src_0','src_1','..., dimensions={0}, use_global_device_ids=true | all-gather | bytes 99840 | tf_op jit(solution)/shard_map/all_gather | solution.py:28
  341.6 30.9 %all-gather.1 = f32[128,3,128]{2,0,1:T(8,128)S(1)} all-gather(f32[64,3,128]{2,0,1:T(8,128)S(1)} %copy.31), channel_id=3, replica_groups=mesh['src_0'=8,'src_1'=4,'src_2'=2,'src_3'=2,'tgt'=2] {'src_3'}, dimensions={0}, use_global_device_ids=true | all-gather | bytes 294912 | tf_op jit(solution)/shard_map/all_gather | solution.py:28
  373.1 31.6 %while.82 = (s32[]{:T(128)}, f32[3,256]{1,0:T(4,128)S(1)}, f32[3,256]{1,0:T(4,128)S(1)}, f32[8,3,2048]{2,1,0:T(4,128)S(1)}, f32[8,3,2048]{2,1,0:T(4,128)S(1)}, /*index=5*/s32[]{:T(128)}, s32[]{:T(128)}) while((s32[]{:T(128)}, f32[3,256]{1,0:T(4,128)S(1)}, f32[3,256]{1,0:T(4,128)S(1)}, f32[8,3,2048]{2,1,0:T(4,128)S(1)}, ...), condition=%wide.region_10.11_spmd.clone, body=%wide.region_6.10_spmd.clone.sunk | while | flops 17302272 | bytes 16992344 | solution.py:66
  405.6 11.9 reduce-scatter.13.cloned.1.call-done
  419.0 14.5 %psum.320 = f32[1]{0:T(128)} all-reduce(f32[1]{0:T(128)} %bitcast.20), channel_id=1, replica_groups=mesh['src_0'=8,'src_1'=4,'src_2'=2,'src_3'=2,'tgt'=2] {'src_0'}, use_global_device_ids=true, to_apply=%region_13.14 | all-reduce | flops 1 | bytes 8 | tf_op jit(solution)/shard_map/psum | solution.py:40
  464.7 11.9 psum.325
  505.7 125.2 %all-gather.12 = f32[64,3,128]{2,1,0:T(4,128)S(1)} all-gather(f32[1,3,128]{2,1,0:T(4,128)S(1)} %multiply_bitcast_fusion.2), channel_id=6, replica_groups=mesh['src_0'=8,'src_1'=4,'src_2'=2,'src_3'=2,'tgt'=2] {'src_0','src_1','..., dimensions={0}, use_global_device_ids=true | all-gather | bytes 99840 | tf_op jit(solution)/shard_map/all_gather | solution.py:28
  630.9 30.9 %all-gather.5 = f32[128,3,128]{2,0,1:T(8,128)S(1)} all-gather(f32[64,3,128]{2,0,1:T(8,128)S(1)} %copy.37), channel_id=7, replica_groups=mesh['src_0'=8,'src_1'=4,'src_2'=2,'src_3'=2,'tgt'=2] {'src_3'}, dimensions={0}, use_global_device_ids=true | all-gather | bytes 294912 | tf_op jit(solution)/shard_map/all_gather | solution.py:28
  662.2 31.6 %while.83 = (s32[]{:T(128)}, f32[3,256]{1,0:T(4,128)S(1)}, f32[3,256]{1,0:T(4,128)S(1)}, f32[8,3,2048]{2,1,0:T(4,128)S(1)}, f32[8,3,2048]{2,1,0:T(4,128)S(1)}, /*index=5*/s32[]{:T(128)}, s32[]{:T(128)}) while((s32[]{:T(128)}, f32[3,256]{1,0:T(4,128)S(1)}, f32[3,256]{1,0:T(4,128)S(1)}, f32[8,3,2048]{2,1,0:T(4,128)S(1)}, ...), condition=%wide.region_29.0_spmd.clone, body=%wide.region_25.29_spmd.clone.sunk | while | flops 17302272 | bytes 16992344 | solution.py:66
  707.4 13.9 psum.330
  749.5 11.9 psum.335
  789.9 125.2 %all-gather.13 = f32[64,3,128]{2,1,0:T(4,128)S(1)} all-gather(f32[1,3,128]{2,1,0:T(4,128)S(1)} %multiply_bitcast_fusion.1), channel_id=8, replica_groups=mesh['src_0'=8,'src_1'=4,'src_2'=2,'src_3'=2,'tgt'=2] {'src_0','src_1','..., dimensions={0}, use_global_device_ids=true | all-gather | bytes 99840 | tf_op jit(solution)/shard_map/all_gather | solution.py:28
  915.1 31.1 %all-gather.7 = f32[128,3,128]{2,0,1:T(8,128)S(1)} all-gather(f32[64,3,128]{2,0,1:T(8,128)S(1)} %copy.40), channel_id=9, replica_groups=mesh['src_0'=8,'src_1'=4,'src_2'=2,'src_3'=2,'tgt'=2] {'src_3'}, dimensions={0}, use_global_device_ids=true | all-gather | bytes 294912 | tf_op jit(solution)/shard_map/all_gather | solution.py:28
  946.6 31.6 %while.84 = (s32[]{:T(128)}, f32[3,256]{1,0:T(4,128)S(1)}, f32[3,256]{1,0:T(4,128)S(1)}, f32[8,3,2048]{2,1,0:T(4,128)S(1)}, f32[8,3,2048]{2,1,0:T(4,128)S(1)}, /*index=5*/s32[]{:T(128)}, s32[]{:T(128)}) while((s32[]{:T(128)}, f32[3,256]{1,0:T(4,128)S(1)}, f32[3,256]{1,0:T(4,128)S(1)}, f32[8,3,2048]{2,1,0:T(4,128)S(1)}, ...), condition=%wide.region_49.0_spmd.clone, body=%wide.region_45.49_spmd.clone.sunk | while | flops 17302272 | bytes 16992344 | solution.py:66
  991.8 13.9 psum.340
  1035.7 11.9 psum.345
  1077.1 125.2 %all-gather.14 = f32[64,3,128]{2,1,0:T(4,128)S(1)} all-gather(f32[1,3,128]{2,1,0:T(4,128)S(1)} %multiply_bitcast_fusion), channel_id=10, replica_groups=mesh['src_0'=8,'src_1'=4,'src_2'=2,'src_3'=2,'tgt'=2] {'src_0','src_1','..., dimensions={0}, use_global_device_ids=true | all-gather | bytes 99840 | tf_op jit(solution)/shard_map/all_gather | solution.py:28
  1202.4 30.9 %all-gather.9 = f32[128,3,128]{2,0,1:T(8,128)S(1)} all-gather(f32[64,3,128]{2,0,1:T(8,128)S(1)} %copy.43), channel_id=11, replica_groups=mesh['src_0'=8,'src_1'=4,'src_2'=2,'src_3'=2,'tgt'=2] {'src_3'}, dimensions={0}, use_global_device_ids=true | all-gather | bytes 294912 | tf_op jit(solution)/shard_map/all_gather | solution.py:28
  1233.7 31.6 %while.85 = (s32[]{:T(128)}, f32[3,256]{1,0:T(4,128)S(1)}, f32[3,256]{1,0:T(4,128)S(1)}, f32[8,3,2048]{2,1,0:T(4,128)S(1)}, f32[8,3,2048]{2,1,0:T(4,128)S(1)}, /*index=5*/s32[]{:T(128)}, s32[]{:T(128)}) while((s32[]{:T(128)}, f32[3,256]{1,0:T(4,128)S(1)}, f32[3,256]{1,0:T(4,128)S(1)}, f32[8,3,2048]{2,1,0:T(4,128)S(1)}, ...), condition=%wide.region_69.70_spmd.clone, body=%wide.region_65.69_spmd.clone.sunk | while | flops 17302272 | bytes 16992344 | solution.py:66
  1278.9 13.9 psum.350
  1324.3 11.9 psum.355
  (323 shorter events, 456.9 us)
Async XLA Ops:
  7.2 410.3 %reduce-scatter.13.cloned.1.call-start = ((), (), s32[]{:S(2)}) async-start(), calls=%async_computation.4 | async-start | bytes 196608
  373.1 45.3 %copy-start.1 = (f32[3,128]{1,0:T(4,128)S(1)}, f32[3,128]{1,0:T(4,128)}, u32[]{:S(2)}) copy-start(f32[3,128]{1,0:T(4,128)} %param.73) | copy-start | bytes 4612
  405.5 300.8 %reduce-scatter.15.cloned.1.call-start = ((), (), s32[]{:S(2)}) async-start(), calls=%async_computation.5 | async-start | bytes 196608
  694.7 296.1 %reduce-scatter.17.cloned.1.call-start = ((), (), s32[]{:S(2)}) async-start(), calls=%async_computation.6 | async-start | bytes 196608
  946.6 59.0 %copy-start.3 = (s32[2]{0:T(128)S(1)}, s32[2]{0:T(128)}, u32[]{:S(2)}) copy-start(s32[2]{0:T(128)} %constant.812.clone.1) | copy-start | bytes 28
  946.6 68.1 %copy-start.2 = (s32[2]{0:T(128)S(1)}, s32[2]{0:T(128)}, u32[]{:S(2)}) copy-start(s32[2]{0:T(128)} %constant.813.clone.1) | copy-start | bytes 28
  979.1 298.7 %reduce-scatter.19.cloned.1.call-start = ((), (), s32[]{:S(2)}) async-start(), calls=%async_computation.7 | async-start | bytes 196608
  1371.7 31.7 %copy-start = (f32[5,4]{0,1:T(4,128)}, f32[5,4]{0,1:T(4,128)S(1)}, u32[]{:S(2)}) copy-start(f32[5,4]{0,1:T(4,128)S(1)} %scatter.61) | copy-start | bytes 244
Sparse Core Ops, SparseCore 0:
  405.7 11.7 reduce-scatter.12
  694.8 11.5 reduce-scatter.14
  979.2 11.4 reduce-scatter.16
  1266.2 11.4 reduce-scatter.18
where the time goes:
time: 1410 us
  blocking collectives  1160 us (82%)
  other arithmetic  143 us (10%)
  waiting for transfers between devices  45 us (3%)
  between operations  40 us (3%)
  local copies, waits for them, and re-layouts  22.1 us (2%)
    all_gather x10, blocking collectives, all_blocks(): parts = lax.all_gather(parts, axes[k])  778 us
    psum x45, blocking collectives, one_axis_at_a_time(): return functools.reduce(lax.psum, axes, value)  375 us
    reduce_sum x32, other arithmetic, stokes_block(): jnp.sum(factor[None] * ((square + soften)[None] * densities[:, None, :] +...  51.7 us
    reduce_sum x32, other arithmetic, stokes_block(): square = jnp.sum(offset * offset, axis=0) + soften  46.3 us
    unnamed x8, waiting for transfers between devices  45 us
  transfers between devices with their start and end apart: 4, of which 4 were waited for; matrix products, arithmetic and copies ran while one was open for 0% of the time, Pallas kernels for 0%

commit v1 on v0

v1 whole, which is shorter than its diff:
```python
import functools

import jax
import jax.numpy as jnp
from jax import lax
from jax.experimental import pallas as pl
from jax.experimental.pallas import tpu as pltpu
from jax.sharding import Mesh
from jax.sharding import PartitionSpec as P

ITERS = 4
soften = 0.0025
LANES = 128
DEPTH = 8
PLANE = 32
MESH = pl.DeviceIdType.MESH
F32 = jnp.float32
BF16 = jnp.bfloat16


def split3(value):
    first = value.astype(BF16).astype(F32)
    rest = value - first
    second = rest.astype(BF16).astype(F32)
    return first, second, rest - second


def row_iota(rows):
    return lax.broadcasted_iota(jnp.int32, (rows, LANES), 0)


def total_of(value):
    return jnp.sum(jnp.sum(value, axis=0, keepdims=True), axis=1, keepdims=True)


def least_squares(columns, heights, beta):
    zero = jnp.zeros_like(beta)
    size = len(columns)
    table = [[zero] * size for _ in range(size + 1)]
    for k in range(size):
        for i in range(k + 1):
            table[i][k] = columns[k][i]
        table[k + 1][k] = heights[k]
    target = [beta] + [zero] * size
    for c in range(size):
        lead, second = table[c][c], table[c + 1][c]
        radius = jnp.sqrt(lead * lead + second * second)
        cosine, sine = lead / radius, second / radius
        top, low = table[c], table[c + 1]
        new_top = [cosine * t + sine * l for t, l in zip(top, low)]
        new_low = [cosine * l - sine * t for t, l in zip(top, low)]
        table[c], table[c + 1] = new_top, new_low
        a, b = target[c], target[c + 1]
        target[c], target[c + 1] = cosine * a + sine * b, cosine * b - sine * a
    y = [zero] * size
    for r in reversed(range(size)):
        partial = zero
        for c in range(r + 1, size):
            partial = partial + table[r][c] * y[c]
        y[r] = (target[r] - partial) / table[r][r]
    return y


def kernel(
    pos_ref, area_ref, rhs_ref, sol_ref, res_ref, hes_ref,
    plane_in, column_in, matrix, sf, tf, coef, phi, psi,
    plane_w, column_p, plane_u, column_u, norm_in, hes, inverse,
    send_sem, plane_sem, column_sem, norm_sem,
):
    my_z = lax.axis_index("z")
    my_p = lax.axis_index("p")
    sources = PLANE * LANES

    def plane_peer(step):
        return (my_z, lax.rem(my_p + step, PLANE))

    def column_peer(step):
        return (lax.rem(my_z + step, DEPTH), my_p)

    barrier = pltpu.get_barrier_semaphore()

    def greet_plane(step, carry):
        pl.semaphore_signal(barrier, inc=1, device_id=plane_peer(step), device_id_type=MESH)
        return carry

    def greet_column(step, carry):
        pl.semaphore_signal(barrier, inc=1, device_id=column_peer(step), device_id_type=MESH)
        return carry

    lax.fori_loop(1, PLANE, greet_plane, 0)
    lax.fori_loop(1, DEPTH, greet_column, 0)
    own = jnp.concatenate(
        [pos_ref[...], area_ref[...], rhs_ref[...], jnp.zeros((1, LANES), F32)], axis=0
    )
    plane_in[my_p] = own
    column_in[my_z] = own
    hes[...] = jnp.zeros_like(hes)
    inverse[...] = jnp.zeros_like(inverse)
    plane_u[...] = jnp.zeros_like(plane_u)
    column_u[...] = jnp.zeros_like(column_u)
    pl.semaphore_wait(barrier, PLANE - 1 + DEPTH - 1)

    def to_plane(ref, recv_sem, slot):
        def send(step, carry):
            pltpu.make_async_remote_copy(
                src_ref=ref.at[my_p], dst_ref=ref.at[my_p],
                send_sem=send_sem.at[slot], recv_sem=recv_sem,
                device_id=plane_peer(step), device_id_type=MESH,
            ).start()
            return carry
        lax.fori_loop(1, PLANE, send, 0, unroll=True)

    def to_column(ref, recv_sem, slot):
        def send(step, carry):
            pltpu.make_async_remote_copy(
                src_ref=ref.at[my_z], dst_ref=ref.at[my_z],
                send_sem=send_sem.at[slot], recv_sem=recv_sem,
                device_id=column_peer(step), device_id_type=MESH,
            ).start()
            return carry
        lax.fori_loop(1, DEPTH, send, 0, unroll=True)

    def all_of(ref, count, recv_sem, slot):
        part = ref.at[pl.ds(0, count - 1)]
        return pltpu.make_async_remote_copy(
            src_ref=part, dst_ref=part, send_sem=send_sem.at[slot], recv_sem=recv_sem,
            device_id=(my_z, my_p), device_id_type=MESH,
        )

    to_column(column_in, column_sem.at[ITERS], 0)
    to_plane(plane_in, plane_sem.at[ITERS], 1)

    all_of(column_in, DEPTH, column_sem.at[ITERS], 0).wait()
    rows8, rows16 = row_iota(8), row_iota(16)
    for t in range(DEPTH):
        block = column_in[t]
        lanes = pl.ds(t * LANES, LANES)
        x = [block[b:b + 1] for b in range(3)]
        square = x[0] * x[0] + x[1] * x[1] + x[2] * x[2]
        feature = jnp.where(
            rows8 < 3, -2.0 * block,
            jnp.where(rows8 == 3, 1.0, jnp.where(rows8 == 4, square + soften, 0.0)),
        )
        t1, t2, t3 = split3(feature)
        tf[0:16, lanes] = jnp.concatenate([t1, t1], axis=0).astype(BF16)
        tf[16:32, lanes] = jnp.concatenate([t2, t1], axis=0).astype(BF16)
        tf[32:48, lanes] = jnp.concatenate([t3, t2], axis=0).astype(BF16)
        for a in range(3):
            value = jnp.zeros((16, LANES), F32)
            for b in range(3):
                value = jnp.where(rows16 == b, x[a] * x[b] + (square if a == b else 0.0), value)
                for c in range(3):
                    part = jnp.zeros((1, LANES), F32)
                    if c == a:
                        part = part - 2.0 * x[b]
                    if b == c:
                        part = part - x[a]
                    if b == a:
                        part = part - x[c]
                    value = jnp.where(rows16 == 3 + 3 * b + c, part, value)
            phi[a, :, lanes] = jnp.where(rows16 == 12 + a, 1.0, value)
            column_u[0, a * DEPTH + t:a * DEPTH + t + 1, :] = block[4 + a:5 + a]

    all_of(plane_in, PLANE, plane_sem.at[ITERS], 1).wait()
    scale = float(PLANE * DEPTH * LANES) ** (-0.5)

    def one_source_block(s, carry):
        block = plane_in[s]
        lanes = pl.ds(pl.multiple_of(s * LANES, LANES), LANES)
        y = [block[b:b + 1] for b in range(3)]
        weight = block[3:4] * scale
        square = y[0] * y[0] + y[1] * y[1] + y[2] * y[2]
        feature = jnp.where(
            rows8 < 3, block, jnp.where(rows8 == 3, square, jnp.where(rows8 == 4, 1.0, 0.0))
        )
        m1, m2, m3 = split3(feature)
        sf[0:16, lanes] = jnp.concatenate([m1, m2], axis=0).astype(BF16)
        sf[16:32, lanes] = jnp.concatenate([m1, m3], axis=0).astype(BF16)
        sf[32:48, lanes] = jnp.concatenate([m1, m2], axis=0).astype(BF16)
        chosen = jnp.zeros((16, LANES), F32)
        for b in range(3):
            mine = ((rows16 >= 3 + 3 * b) & (rows16 < 6 + 3 * b)) | (rows16 == 12 + b)
            chosen = jnp.where(mine, y[b], chosen)
        for b in range(3):
            linear = (rows16 == 3 + b) | (rows16 == 6 + b) | (rows16 == 9 + b)
            last = (rows16 >= 12) & (rows16 < 15)
            value = jnp.where(
                rows16 == b, 1.0, jnp.where(linear, chosen, jnp.where(last, chosen * y[b], 0.0))
            )
            value = value + jnp.where(rows16 == 12 + b, square + 2.0 * soften, 0.0)
            coef[b, :, lanes] = value * weight
        plane_u[0, s] = block[4:8]
        return carry

    lax.fori_loop(0, PLANE, one_source_block, 0)

    chunk = 512

    def factor_block(t, carry):
        targets = tf[:, pl.ds(pl.multiple_of(t * LANES, LANES), LANES)]
        for s in range(sources // chunk):
            lanes = slice(s * chunk, (s + 1) * chunk)
            square = lax.dot_general(
                targets, sf[:, lanes], (((0,), (0,)), ((), ())), preferred_element_type=F32
            )
            root = lax.rsqrt(square)
            factor = root * root * root
            high = factor.astype(BF16)
            matrix[t, 0:LANES, lanes] = high
            matrix[t, LANES:2 * LANES, lanes] = (factor - high.astype(F32)).astype(BF16)
        return carry

    lax.fori_loop(0, DEPTH, factor_block, 0)

    lane_row = lax.broadcasted_iota(jnp.int32, (1, LANES), 1)
    hes_rows, hes_lanes = row_iota(8), lax.broadcasted_iota(jnp.int32, (8, LANES), 1)

    def one_step(k, carry):
        for s in range(PLANE):
            lanes = slice(s * LANES, (s + 1) * LANES)
            block = plane_u[k, s]
            value = (
                coef[0, :, lanes] * block[0:1]
                + coef[1, :, lanes] * block[1:2]
                + coef[2, :, lanes] * block[2:3]
            )
            p1, p2, p3 = split3(value)
            psi[0:16, lanes] = p1.astype(BF16)
            psi[16:32, lanes] = p2.astype(BF16)
            psi[32:48, lanes] = p3.astype(BF16)

        def image_block(t, inner):
            product = lax.dot_general(
                matrix[t], psi[...], (((1,), (1,)), ((), ())), preferred_element_type=F32
            )
            both = product[0:LANES] + product[LANES:2 * LANES]
            turned = both.T
            summed = turned[0:16] + turned[16:32] + turned[32:48]
            lanes = pl.ds(pl.multiple_of(t * LANES, LANES), LANES)
            for a in range(3):
                column_p[k, my_z, pl.ds(a * DEPTH + t, 1), :] = jnp.sum(
                    phi[a, :, lanes] * summed, axis=0, keepdims=True
                )
            return inner

        lax.fori_loop(0, DEPTH, image_block, 0)

        to_column(column_p.at[k], column_sem.at[k], 0)
        latest = column_u[k]
        all_of(column_p.at[k], DEPTH, column_sem.at[k], 0).wait()
        applied = latest
        for z in range(DEPTH):
            applied = applied + column_p[k, z]
        column_u[k + 1] = applied
        message = jnp.where(lane_row == 4, total_of(latest * latest), 0.0)
        for i in range(ITERS):
            message = message + jnp.where(lane_row == i, total_of(column_u[i] * applied), 0.0) * (
                jnp.where(i <= k, 1.0, 0.0)
            )
        for a in range(3):
            plane_w[k, my_p, a:a + 1, :] = column_u[k + 1, pl.ds(a * DEPTH + my_z, 1), :]
        plane_w[k, my_p, 3:4, :] = message
        to_plane(plane_w.at[k], plane_sem.at[k], 1)
        all_of(plane_w.at[k], PLANE, plane_sem.at[k], 1).wait()
        sums = jnp.sum(plane_w[k, :, 3, :], axis=0, keepdims=True)
        norm = jnp.sqrt(sums[:, 4:5])
        scaled = 1.0 / norm
        inverse[pl.ds(k, 1), :] = jnp.broadcast_to(scaled, (1, LANES))
        table = jnp.where((hes_rows == k) & (hes_lanes == k - 1), norm, hes[0:8])
        factors = []
        for i in range(ITERS):
            present = inverse[i:i + 1, 0:1]
            value = sums[:, i:i + 1] * present * scaled
            table = jnp.where((hes_rows == i) & (hes_lanes == k), value, table)
            factors.append(value * present)
        hes[0:8] = table
        hes[8:9] = jnp.where(k == 0, jnp.broadcast_to(norm, (1, LANES)), hes[8:9])
        fresh = applied * scaled
        for i in range(ITERS):
            fresh = fresh - jnp.where(i <= k, factors[i] * column_u[i], 0.0)
        column_u[k + 1] = fresh
        for s in range(PLANE):
            fresh = plane_w[k, s] * scaled
            for i in range(ITERS):
                fresh = fresh - factors[i] * plane_u[i, s]
            plane_u[k + 1, s] = fresh
        return carry

    lax.fori_loop(0, ITERS, one_step, 0)

    last = column_u[ITERS]
    norm_in[my_p] = jnp.broadcast_to(total_of(last * last), (8, LANES))
    to_plane(norm_in, norm_sem, 1)
    all_of(norm_in, PLANE, norm_sem, 1).wait()
    sums = jnp.sum(norm_in[:, 0, :], axis=0, keepdims=True)
    norm = jnp.sqrt(sums[:, 0:1])
    inverse[ITERS:ITERS + 1, :] = jnp.broadcast_to(1.0 / norm, (1, LANES))
    table = jnp.where((hes_rows == ITERS) & (hes_lanes == ITERS - 1), norm, hes[0:8])
    hes_ref[...] = table[0:ITERS + 1, 0:ITERS]
    entry = [[table[i:i + 1, k:k + 1] for k in range(ITERS)] for i in range(ITERS + 1)]
    beta = hes[8:9, 0:1]
    y = least_squares(
        [[entry[i][k] for i in range(k + 1)] for k in range(ITERS)],
        [entry[k + 1][k] for k in range(ITERS)],
        beta,
    )
    for a in range(3):
        solved = jnp.zeros((1, LANES), F32)
        misfit = jnp.zeros((1, LANES), F32)
        for i in range(ITERS + 1):
            basis = column_u[i, pl.ds(a * DEPTH + my_z, 1), :] * inverse[i:i + 1, :]
            if i < ITERS:
                solved = solved + y[i] * basis
            g = beta if i == 0 else jnp.zeros_like(beta)
            for k in range(max(i - 1, 0), ITERS):
                g = g - entry[i][k] * y[k]
            misfit = misfit + g * basis
        sol_ref[a:a + 1, :] = solved
        res_ref[a:a + 1, :] = misfit


def shards(positions, areas, right_side):
    vmem = pl.BlockSpec(memory_space=pltpu.VMEM)
    sources, targets = PLANE * LANES, DEPTH * LANES
    return pl.pallas_call(
        kernel,
        out_shape=(
            jax.ShapeDtypeStruct((3, LANES), F32),
            jax.ShapeDtypeStruct((3, LANES), F32),
            jax.ShapeDtypeStruct((ITERS + 1, ITERS), F32),
        ),
        in_specs=[vmem] * 3,
        out_specs=(vmem,) * 3,
        scratch_shapes=[
            pltpu.VMEM((PLANE, 8, LANES), F32),
            pltpu.VMEM((DEPTH, 8, LANES), F32),
            pltpu.VMEM((DEPTH, 2 * LANES, sources), BF16),
            pltpu.VMEM((48, sources), BF16),
            pltpu.VMEM((48, targets), BF16),
            pltpu.VMEM((3, 16, sources), F32),
            pltpu.VMEM((3, 16, targets), F32),
            pltpu.VMEM((48, sources), BF16),
            pltpu.VMEM((ITERS, PLANE, 4, LANES), F32),
            pltpu.VMEM((ITERS, DEPTH, 3 * DEPTH, LANES), F32),
            pltpu.VMEM((ITERS + 1, PLANE, 4, LANES), F32),
            pltpu.VMEM((ITERS + 1, 3 * DEPTH, LANES), F32),
            pltpu.VMEM((PLANE, 8, LANES), F32),
            pltpu.VMEM((16, LANES), F32),
            pltpu.VMEM((8, LANES), F32),
            pltpu.SemaphoreType.DMA((2,)),
            pltpu.SemaphoreType.DMA((ITERS + 1,)),
            pltpu.SemaphoreType.DMA((ITERS + 1,)),
            pltpu.SemaphoreType.DMA,
        ],
        compiler_params=pltpu.CompilerParams(
            collective_id=0, has_side_effects=True, vmem_limit_bytes=56 * 1024 * 1024
        ),
        name="arnoldi",
    )(positions, areas.reshape(1, -1), right_side)


def solution(mesh):
    split = Mesh(mesh.devices.reshape(DEPTH, PLANE), ("z", "p"))
    return jax.shard_map(
        shards,
        mesh=split,
        in_specs=(P(None, ("z", "p")), P(("z", "p")), P(None, ("z", "p"))),
        out_specs=(P(None, ("z", "p")), P(None, ("z", "p")), P()),
        check_vma=False,
    )
```

time: 1410 us -> 101 us (0.07)
  blocking collectives: 1160 us -> 0 us
  other arithmetic: 143 us -> 0 us
  Pallas kernels: 0 us -> 97.4 us
  waiting for transfers between devices: 45 us -> 0 us
  between operations: 40 us -> 0.65 us
  local copies, waits for them, and re-layouts: 22.1 us -> 2.59 us
    all_gather x11 -> x0, blocking collectives: 783 us -> none  [the longest x10 778 us: all_blocks(): parts = lax.all_gather(parts, axes[k])]
    psum x45 -> x0, blocking collectives: 375 us -> none  [one_axis_at_a_time(): return functools.reduce(lax.psum, axes, value)]
    reduce_sum x80 -> x0, other arithmetic: 106 us -> none  [the longest x32 51.7 us: stokes_block(): jnp.sum(factor[None] * ((square + soften)[None] * densities[:, None, :] +...]
    pallas_call x0 -> x1, Pallas kernels: none -> 97.4 us  [shards(): pl.pallas_call(kernel, out_shape=(jax.ShapeDtypeStruct((3, LANES), F32),...]
    unnamed x8 -> x0, waiting for transfers between devices: 45 us -> none
    pow x32 -> x0, other arithmetic: 26.1 us -> none  [stokes_block(): factor = square ** (-1.5)]
  transfers between devices with their start and end apart: 4 -> 0, of which waited for: 4 -> 0; matrix products, arithmetic and copies ran while one was open for 0% -> 0% of each run, Pallas kernels for 0% -> 0%
where the time goes in v1:
time: 101 us
  Pallas kernels  97.4 us (96%)
  local copies, waits for them, and re-layouts  2.59 us (3%)
    pallas_call x1, Pallas kernels, shards(): pl.pallas_call(kernel, out_shape=(jax.ShapeDtypeStruct((3, LANES), F32),...  97.4 us

profile of v1, /device:TPU:1, one launch (start us, length us, event | category | flops | bytes accessed | tf_op | source)
XLA Modules:
  0.0 100.7 jit_solution(519297276143389547)
XLA Ops:
  0.6 97.4 %arnoldi.1 = (f32[3,128]{1,0:T(4,128)}, f32[3,128]{1,0:T(4,128)}, f32[5,4]{1,0:T(8,128)}) custom-call(f32[3,128]{1,0:T(4,128)} %pos_ref.1, f32[1,128]{1,0:T(1,128)} %bitcast.1, f32[3,128]{1,0:T(4,128)} %rhs_ref.1), custom_call_target="tpu_custom_call" | custom-call | tf_op jit(solution)/shard_map/arnoldi/pallas_call | solution.py:325
  98.0 0.0 copy-start
  98.1 0.7 copy-done
  98.7 0.0 copy-start.2
  98.7 0.7 copy.6
  99.4 0.0 copy-done.2
  99.4 0.0 copy-start.1
  99.4 0.6 copy.9
  100.0 0.1 copy-done.1
  100.1 0.6 copy.10
Async XLA Ops:
  98.0 0.7 copy-start
  98.7 0.7 copy-start.2
  99.4 0.7 copy-start.1

commit v2 on v1

--- a/solution.py
+++ b/solution.py
@@ -11,8 +11,11 @@
 ITERS = 4
 soften = 0.0025
 LANES = 128
+WIDE = 256
+CHUNK = 256
 DEPTH = 8
 PLANE = 32
+BLOCKS = DEPTH * LANES // WIDE
 MESH = pl.DeviceIdType.MESH
 F32 = jnp.float32
 BF16 = jnp.bfloat16
@@ -62,10 +65,10 @@
 
 
 def kernel(
-    pos_ref, area_ref, rhs_ref, sol_ref, res_ref, hes_ref,
+    pos_ref, area_ref, rhs_ref, packed_ref,
     plane_in, column_in, matrix, sf, tf, coef, phi, psi,
-    plane_w, column_p, plane_u, column_u, norm_in, hes, inverse,
-    send_sem, plane_sem, column_sem, norm_sem,
+    plane_w, column_p, plane_u, column_u, gram, hes, inverse,
+    send_sem, plane_sem, column_sem,
 ):
     my_z = lax.axis_index("z")
     my_p = lax.axis_index("p")
@@ -194,23 +197,21 @@
 
     lax.fori_loop(0, PLANE, one_source_block, 0)
 
-    chunk = 512
-
-    def factor_block(t, carry):
-        targets = tf[:, pl.ds(pl.multiple_of(t * LANES, LANES), LANES)]
-        for s in range(sources // chunk):
-            lanes = slice(s * chunk, (s + 1) * chunk)
+    def factor_block(s, carry):
+        rows = pl.ds(pl.multiple_of(s * CHUNK, CHUNK), CHUNK)
+        for b in range(BLOCKS):
             square = lax.dot_general(
-                targets, sf[:, lanes], (((0,), (0,)), ((), ())), preferred_element_type=F32
+                sf[:, rows], tf[:, b * WIDE:(b + 1) * WIDE], (((0,), (0,)), ((), ())),
+                preferred_element_type=F32,
             )
             root = lax.rsqrt(square)
             factor = root * root * root
             high = factor.astype(BF16)
-            matrix[t, 0:LANES, lanes] = high
-            matrix[t, LANES:2 * LANES, lanes] = (factor - high.astype(F32)).astype(BF16)
-        return carry
-
-    lax.fori_loop(0, DEPTH, factor_block, 0)
+            matrix[b, rows, 0:WIDE] = high
+            matrix[b, rows, WIDE:2 * WIDE] = (factor - high.astype(F32)).astype(BF16)
+        return carry
+
+    lax.fori_loop(0, sources // CHUNK, factor_block, 0)
 
     lane_row = lax.broadcasted_iota(jnp.int32, (1, LANES), 1)
     hes_rows, hes_lanes = row_iota(8), lax.broadcasted_iota(jnp.int32, (8, LANES), 1)
@@ -229,41 +230,44 @@
             psi[16:32, lanes] = p2.astype(BF16)
             psi[32:48, lanes] = p3.astype(BF16)
 
-        def image_block(t, inner):
+        for b in range(BLOCKS):
             product = lax.dot_general(
-                matrix[t], psi[...], (((1,), (1,)), ((), ())), preferred_element_type=F32
-            )
-            both = product[0:LANES] + product[LANES:2 * LANES]
-            turned = both.T
-            summed = turned[0:16] + turned[16:32] + turned[32:48]
-            lanes = pl.ds(pl.multiple_of(t * LANES, LANES), LANES)
+                psi[...], matrix[b], (((1,), (0,)), ((), ())), preferred_element_type=F32
+            )
+            both = product[:, 0:WIDE] + product[:, WIDE:2 * WIDE]
+            summed = both[0:16] + both[16:32] + both[32:48]
             for a in range(3):
-                column_p[k, my_z, pl.ds(a * DEPTH + t, 1), :] = jnp.sum(
-                    phi[a, :, lanes] * summed, axis=0, keepdims=True
+                row = jnp.sum(
+                    phi[a, :, b * WIDE:(b + 1) * WIDE] * summed, axis=0, keepdims=True
                 )
-            return inner
-
-        lax.fori_loop(0, DEPTH, image_block, 0)
+                for c in range(WIDE // LANES):
+                    t = b * (WIDE // LANES) + c
+                    column_p[k, my_z, a * DEPTH + t:a * DEPTH + t + 1, :] = (
+                        row[:, c * LANES:(c + 1) * LANES]
+                    )
 
         to_column(column_p.at[k], column_sem.at[k], 0)
         latest = column_u[k]
+        message = jnp.where(lane_row == 6, total_of(latest * latest), 0.0)
+        for i in range(ITERS):
+            part = jnp.where(lane_row == 8 + i, total_of(column_u[i] * latest), 0.0)
+            message = message + part
         all_of(column_p.at[k], DEPTH, column_sem.at[k], 0).wait()
         applied = latest
         for z in range(DEPTH):
             applied = applied + column_p[k, z]
+        message = message + jnp.where(lane_row == 4, total_of(applied * applied), 0.0)
+        for i in range(ITERS):
+            message = message + jnp.where(lane_row == i, total_of(column_u[i] * applied), 0.0)
         column_u[k + 1] = applied
-        message = jnp.where(lane_row == 4, total_of(latest * latest), 0.0)
-        for i in range(ITERS):
-            message = message + jnp.where(lane_row == i, total_of(column_u[i] * applied), 0.0) * (
-                jnp.where(i <= k, 1.0, 0.0)
-            )
         for a in range(3):
             plane_w[k, my_p, a:a + 1, :] = column_u[k + 1, pl.ds(a * DEPTH + my_z, 1), :]
         plane_w[k, my_p, 3:4, :] = message
         to_plane(plane_w.at[k], plane_sem.at[k], 1)
         all_of(plane_w.at[k], PLANE, plane_sem.at[k], 1).wait()
         sums = jnp.sum(plane_w[k, :, 3, :], axis=0, keepdims=True)
-        norm = jnp.sqrt(sums[:, 4:5])
+        gram[pl.ds(k, 1), :] = sums
+        norm = jnp.sqrt(sums[:, 6:7])
         scaled = 1.0 / norm
         inverse[pl.ds(k, 1), :] = jnp.broadcast_to(scaled, (1, LANES))
         table = jnp.where((hes_rows == k) & (hes_lanes == k - 1), norm, hes[0:8])
@@ -288,15 +292,20 @@
 
     lax.fori_loop(0, ITERS, one_step, 0)
 
-    last = column_u[ITERS]
-    norm_in[my_p] = jnp.broadcast_to(total_of(last * last), (8, LANES))
-    to_plane(norm_in, norm_sem, 1)
-    all_of(norm_in, PLANE, norm_sem, 1).wait()
-    sums = jnp.sum(norm_in[:, 0, :], axis=0, keepdims=True)
-    norm = jnp.sqrt(sums[:, 0:1])
+    present = [inverse[i:i + 1, 0:1] for i in range(ITERS)]
+    tall = [hes[i:i + 1, ITERS - 1:ITERS] for i in range(ITERS)]
+    whole = gram[ITERS - 1:ITERS, 4:5] * present[-1] * present[-1]
+    square = whole
+    for i in range(ITERS):
+        square = square - tall[i] * tall[i]
+        for j in range(i + 1, ITERS):
+            square = square + 2.0 * (tall[i] * present[i]) * (tall[j] * present[j]) * (
+                gram[j:j + 1, 8 + i:9 + i]
+            )
+    norm = jnp.sqrt(jnp.maximum(square, whole * 1e-14))
     inverse[ITERS:ITERS + 1, :] = jnp.broadcast_to(1.0 / norm, (1, LANES))
     table = jnp.where((hes_rows == ITERS) & (hes_lanes == ITERS - 1), norm, hes[0:8])
-    hes_ref[...] = table[0:ITERS + 1, 0:ITERS]
+    packed_ref[8:16] = table
     entry = [[table[i:i + 1, k:k + 1] for k in range(ITERS)] for i in range(ITERS + 1)]
     beta = hes[8:9, 0:1]
     y = least_squares(
@@ -315,26 +324,28 @@
             for k in range(max(i - 1, 0), ITERS):
                 g = g - entry[i][k] * y[k]
             misfit = misfit + g * basis
-        sol_ref[a:a + 1, :] = solved
-        res_ref[a:a + 1, :] = misfit
+        packed_ref[a:a + 1, :] = solved
+        packed_ref[4 + a:5 + a, :] = misfit
+
+
+def unpack(packed_ref, sol_ref, res_ref, hes_ref):
+    sol_ref[...] = packed_ref[0:3]
+    res_ref[...] = packed_ref[4:7]
+    hes_ref[...] = packed_ref[8:16].T[0:ITERS, 0:ITERS + 1]
 
 
 def shards(positions, areas, right_side):
     vmem = pl.BlockSpec(memory_space=pltpu.VMEM)
     sources, targets = PLANE * LANES, DEPTH * LANES
-    return pl.pallas_call(
+    packed = pl.pallas_call(
         kernel,
-        out_shape=(
-            jax.ShapeDtypeStruct((3, LANES), F32),
-            jax.ShapeDtypeStruct((3, LANES), F32),
-            jax.ShapeDtypeStruct((ITERS + 1, ITERS), F32),
-        ),
+        out_shape=jax.ShapeDtypeStruct((16, LANES), F32),
         in_specs=[vmem] * 3,
-        out_specs=(vmem,) * 3,
+        out_specs=vmem,
         scratch_shapes=[
             pltpu.VMEM((PLANE, 8, LANES), F32),
             pltpu.VMEM((DEPTH, 8, LANES), F32),
-            pltpu.VMEM((DEPTH, 2 * LANES, sources), BF16),
+            pltpu.VMEM((BLOCKS, sources, 2 * WIDE), BF16),
             pltpu.VMEM((48, sources), BF16),
             pltpu.VMEM((48, targets), BF16),
             pltpu.VMEM((3, 16, sources), F32),
@@ -344,19 +355,30 @@
             pltpu.VMEM((ITERS, DEPTH, 3 * DEPTH, LANES), F32),
             pltpu.VMEM((ITERS + 1, PLANE, 4, LANES), F32),
             pltpu.VMEM((ITERS + 1, 3 * DEPTH, LANES), F32),
-            pltpu.VMEM((PLANE, 8, LANES), F32),
+            pltpu.VMEM((8, LANES), F32),
             pltpu.VMEM((16, LANES), F32),
             pltpu.VMEM((8, LANES), F32),
             pltpu.SemaphoreType.DMA((2,)),
             pltpu.SemaphoreType.DMA((ITERS + 1,)),
             pltpu.SemaphoreType.DMA((ITERS + 1,)),
-            pltpu.SemaphoreType.DMA,
         ],
         compiler_params=pltpu.CompilerParams(
             collective_id=0, has_side_effects=True, vmem_limit_bytes=56 * 1024 * 1024
         ),
         name="arnoldi",
     )(positions, areas.reshape(1, -1), right_side)
+    solved, misfit, turned = pl.pallas_call(
+        unpack,
+        out_shape=(
+            jax.ShapeDtypeStruct((3, LANES), F32),
+            jax.ShapeDtypeStruct((3, LANES), F32),
+            jax.ShapeDtypeStruct((ITERS, ITERS + 1), F32),
+        ),
+        in_specs=[vmem],
+        out_specs=(vmem,) * 3,
+        name="unpack",
+    )(packed)
+    return solved, misfit, turned.T
 
 
 def solution(mesh):

time: 101 us -> 84 us (0.83)
  Pallas kernels: 97.4 us -> 83.2 us
  local copies, waits for them, and re-layouts: 2.59 us -> 0 us
    pallas_call x1 -> x2, Pallas kernels: 97.4 us -> 83.2 us  [the longest x1 81.8 us: shards(): pl.pallas_call(kernel, out_shape=jax.ShapeDtypeStruct((16, LANES), F32),...]
    unnamed x8 -> x0, local copies, waits for them, and re-layouts: 1.93 us -> none
where the time goes in v2:
time: 84 us; the launch traced here: 83.8 us
  Pallas kernels  83.2 us (99%)
    pallas_call x1, Pallas kernels, shards(): pl.pallas_call(kernel, out_shape=jax.ShapeDtypeStruct((16, LANES), F32),...  81.8 us

profile of v2, /device:TPU:1, one launch (start us, length us, event | category | flops | bytes accessed | tf_op | source)
XLA Modules:
  0.0 83.8 jit_solution(17807671488000340352)
XLA Ops:
  0.6 81.8 %arnoldi.1.packed_ref = f32[16,128]{1,0:T(8,128)} custom-call(f32[3,128]{1,0:T(4,128)} %pos_ref.1, f32[1,128]{1,0:T(1,128)} %bitcast.2, f32[3,128]{1,0:T(4,128)} %rhs_ref.1), custom_call_target="tpu_custom_call" | custom-call | tf_op jit(solution)/shard_map/arnoldi/pallas_call | solution.py:340
  82.5 1.3 %unpack.1 = (f32[3,128]{1,0:T(4,128)}, f32[3,128]{1,0:T(4,128)}, f32[4,5]{1,0:T(4,128)}) custom-call(f32[16,128]{1,0:T(8,128)} %arnoldi.1.packed_ref), custom_call_target="tpu_custom_call" | custom-call | tf_op jit(solution)/shard_map/unpack/pallas_call | solution.py:370

commit v3 on v2

v3 whole, which is shorter than its diff:
```python
import functools

import jax
import jax.numpy as jnp
from jax import lax
from jax.experimental import pallas as pl
from jax.experimental.pallas import tpu as pltpu
from jax.sharding import Mesh
from jax.sharding import PartitionSpec as P

ITERS = 4
soften = 0.0025
LANES = 128
WIDE = 256
CHUNK = 512
DEEP = 1024
DEPTH = 8
PLANE = 32
BLOCKS = DEPTH * LANES // WIDE
MESH = pl.DeviceIdType.MESH
F32 = jnp.float32
BF16 = jnp.bfloat16


def split3(value):
    first = value.astype(BF16).astype(F32)
    rest = value - first
    second = rest.astype(BF16).astype(F32)
    return first, second, rest - second


def row_iota(rows):
    return lax.broadcasted_iota(jnp.int32, (rows, LANES), 0)


def total_of(value):
    return jnp.sum(jnp.sum(value, axis=0, keepdims=True), axis=1, keepdims=True)


def least_squares(columns, heights, beta):
    zero = jnp.zeros_like(beta)
    size = len(columns)
    table = [[zero] * size for _ in range(size + 1)]
    for k in range(size):
        for i in range(k + 1):
            table[i][k] = columns[k][i]
        table[k + 1][k] = heights[k]
    target = [beta] + [zero] * size
    for c in range(size):
        lead, second = table[c][c], table[c + 1][c]
        radius = jnp.sqrt(lead * lead + second * second)
        cosine, sine = lead / radius, second / radius
        top, low = table[c], table[c + 1]
        new_top = [cosine * t + sine * l for t, l in zip(top, low)]
        new_low = [cosine * l - sine * t for t, l in zip(top, low)]
        table[c], table[c + 1] = new_top, new_low
        a, b = target[c], target[c + 1]
        target[c], target[c + 1] = cosine * a + sine * b, cosine * b - sine * a
    y = [zero] * size
    for r in reversed(range(size)):
        partial = zero
        for c in range(r + 1, size):
            partial = partial + table[r][c] * y[c]
        y[r] = (target[r] - partial) / table[r][r]
    return y


def kernel(
    pos_ref, area_ref, rhs_ref, packed_ref,
    plane_in, column_in, matrix, sf, tf, coef, phi, psi, image,
    plane_w, column_w, part_out, part_in, part_all, plane_u, column_u, gram, hes, inverse,
    load_sem, send_sem, plane_sem, column_sem, part_sem,
):
    my_z = lax.axis_index("z")
    my_p = lax.axis_index("p")
    my_y, my_x = my_p // 8, (my_p % 2) * 2 + (my_p // 4) % 2
    my_c = (my_p // 2) % 2
    sources = PLANE * LANES

    ys = [((my_y + d) % 4) * 8 for d in range(4)]
    xs = [((my_x + d) % 4) for d in range(4)]
    xs = [(x % 2) * 4 + x // 2 for x in xs]
    cs = [((my_c + d) % 2) * 2 for d in range(2)]
    hops = (0, 1, 2, 1)
    steps = [(a, b, c) for a in range(4) for b in range(4) for c in range(2)][1:]
    steps.sort(key=lambda s: -(4 * (hops[s[0]] + hops[s[1]]) + s[2]))
    plane_peers = [(s[0], (my_z, ys[s[0]] + xs[s[1]] + cs[s[2]])) for s in steps]
    column_peers = [((my_z + d) % DEPTH, my_p) for d in (4, 3, 5, 2, 6, 1, 7)]

    barrier = pltpu.get_barrier_semaphore()
    for device in column_peers + [peer for _, peer in plane_peers]:
        pl.semaphore_signal(barrier, inc=1, device_id=device, device_id_type=MESH)
    own = plane_in.at[my_p]
    loads = [
        pltpu.make_async_copy(pos_ref, own.at[0:3], load_sem.at[0]),
        pltpu.make_async_copy(area_ref, own.at[3:4], load_sem.at[1]),
        pltpu.make_async_copy(rhs_ref, own.at[4:7], load_sem.at[2]),
    ]
    for load in loads:
        load.start()
    plane_in[my_p, 7:8, :] = jnp.zeros((1, LANES), F32)
    hes[...] = jnp.zeros_like(hes)
    inverse[...] = jnp.zeros_like(inverse)
    plane_u[...] = jnp.zeros_like(plane_u)
    column_u[...] = jnp.zeros_like(column_u)
    part_out[...] = jnp.zeros_like(part_out)
    for load in loads:
        load.wait()
    pl.semaphore_wait(barrier, PLANE - 1 + DEPTH - 1)

    def send(src, dst, device, slot, recv_sem):
        pltpu.make_async_remote_copy(
            src_ref=src, dst_ref=dst, send_sem=send_sem.at[slot], recv_sem=recv_sem,
            device_id=device, device_id_type=MESH,
        ).start()

    def arrived(part, recv_sem):
        pltpu.make_async_remote_copy(
            src_ref=part, dst_ref=part, send_sem=send_sem.at[0], recv_sem=recv_sem,
            device_id=(my_z, my_p), device_id_type=MESH,
        ).wait_recv()

    def sent(part, slot):
        pltpu.make_async_remote_copy(
            src_ref=part, dst_ref=part, send_sem=send_sem.at[slot], recv_sem=load_sem.at[0],
            device_id=(my_z, my_p), device_id_type=MESH,
        ).wait_send()

    for device in column_peers:
        send(own, column_in.at[my_z], device, 0, column_sem.at[ITERS])
    for turn, device in plane_peers:
        send(own, own, device, 1, plane_sem.at[ITERS + (4 - turn) % 4])
    column_in[my_z] = plane_in[my_p]

    rows8, rows16 = row_iota(8), row_iota(16)
    scale = float(PLANE * DEPTH * LANES) ** (-0.5)

    def one_source_block(s):
        block = plane_in[s]
        lanes = pl.ds(pl.multiple_of(s * LANES, LANES), LANES)
        y = [block[b:b + 1] for b in range(3)]
        weight = block[3:4] * scale
        square = y[0] * y[0] + y[1] * y[1] + y[2] * y[2]
        feature = jnp.where(
            rows8 < 3, block, jnp.where(rows8 == 3, square, jnp.where(rows8 == 4, 1.0, 0.0))
        )
        m1, m2, m3 = split3(feature)
        sf[0:16, lanes] = jnp.concatenate([m1, m2], axis=0).astype(BF16)
        sf[16:32, lanes] = jnp.concatenate([m1, m3], axis=0).astype(BF16)
        sf[32:48, lanes] = jnp.concatenate([m1, m2], axis=0).astype(BF16)
        chosen = jnp.zeros((16, LANES), F32)
        for b in range(3):
            mine = ((rows16 >= 3 + 3 * b) & (rows16 < 6 + 3 * b)) | (rows16 == 12 + b)
            chosen = jnp.where(mine, y[b], chosen)
        total = jnp.zeros((16, LANES), F32)
        for b in range(3):
            linear = (rows16 == 3 + b) | (rows16 == 6 + b) | (rows16 == 9 + b)
            last = (rows16 >= 12) & (rows16 < 15)
            value = jnp.where(
                rows16 == b, 1.0, jnp.where(linear, chosen, jnp.where(last, chosen * y[b], 0.0))
            )
            value = value + jnp.where(rows16 == 12 + b, square + 2.0 * soften, 0.0)
            value = value * weight
            coef[b, :, lanes] = value
            total = total + value * block[4 + b:5 + b]
        for piece, part in enumerate(split3(total)):
            psi[16 * piece:16 * piece + 16, lanes] = part.astype(BF16)
        plane_u[0, s] = block[4:8]

    def source_rows(turn, count):
        arrived(plane_in.at[pl.ds(0, count)], plane_sem.at[ITERS + turn])
        first = ((my_y + turn) % 4) * 8

        def body(s, carry):
            one_source_block(first + s)
            return carry

        lax.fori_loop(0, 8, body, 0)

    source_rows(0, 7)
    source_rows(1, 8)
    source_rows(3, 8)

    arrived(column_in.at[pl.ds(0, DEPTH - 1)], column_sem.at[ITERS])
    for t in range(DEPTH):
        block = column_in[t]
        lanes = pl.ds(t * LANES, LANES)
        x = [block[b:b + 1] for b in range(3)]
        square = x[0] * x[0] + x[1] * x[1] + x[2] * x[2]
        feature = jnp.where(
            rows8 < 3, -2.0 * block,
            jnp.where(rows8 == 3, 1.0, jnp.where(rows8 == 4, square + soften, 0.0)),
        )
        t1, t2, t3 = split3(feature)
        tf[0:16, lanes] = jnp.concatenate([t1, t1], axis=0).astype(BF16)
        tf[16:32, lanes] = jnp.concatenate([t2, t1], axis=0).astype(BF16)
        tf[32:48, lanes] = jnp.concatenate([t3, t2], axis=0).astype(BF16)
        for a in range(3):
            value = jnp.zeros((16, LANES), F32)
            for b in range(3):
                value = jnp.where(rows16 == b, x[a] * x[b] + (square if a == b else 0.0), value)
                for c in range(3):
                    part = jnp.zeros((1, LANES), F32)
                    if c == a:
                        part = part - 2.0 * x[b]
                    if b == c:
                        part = part - x[a]
                    if b == a:
                        part = part - x[c]
                    value = jnp.where(rows16 == 3 + 3 * b + c, part, value)
            phi[a, :, lanes] = jnp.where(rows16 == 12 + a, 1.0, value)
        column_u[0, t] = block[4:8]

    source_rows(2, 8)

    image[...] = jnp.zeros_like(image)

    def factor_block(s, carry):
        rows = pl.ds(pl.multiple_of(s * CHUNK, CHUNK), CHUNK)
        left = psi[:, rows]
        for b in range(BLOCKS):
            square = lax.dot_general(
                sf[:, rows], tf[:, b * WIDE:(b + 1) * WIDE], (((0,), (0,)), ((), ())),
                preferred_element_type=F32,
            )
            root = lax.rsqrt(square)
            factor = root * root * root
            high = factor.astype(BF16)
            low = (factor - high.astype(F32)).astype(BF16)
            matrix[b, rows, 0:WIDE] = high
            matrix[b, rows, WIDE:2 * WIDE] = low
            image[:, b * WIDE:(b + 1) * WIDE] += jnp.dot(
                left, high, preferred_element_type=F32
            ) + jnp.dot(left, low, preferred_element_type=F32)
        return carry

    lax.fori_loop(0, sources // CHUNK, factor_block, 0)

    def to_parts(k, b, both):
        summed = both[0:16] + both[16:32] + both[32:48]
        for a in range(3):
            row = jnp.sum(phi[a, :, b * WIDE:(b + 1) * WIDE] * summed, axis=0, keepdims=True)
            for c in range(WIDE // LANES):
                part_out[k, b * (WIDE // LANES) + c, a:a + 1, :] = (
                    row[:, c * LANES:(c + 1) * LANES]
                )

    for b in range(BLOCKS):
        to_parts(0, b, image[:, b * WIDE:(b + 1) * WIDE])

    lane_row = lax.broadcasted_iota(jnp.int32, (1, LANES), 1)
    hes_rows, hes_lanes = row_iota(8), lax.broadcasted_iota(jnp.int32, (8, LANES), 1)

    def inner(left, right):
        return total_of(jnp.sum(left * right, axis=0)[0:3])

    def at_lane(lane, value):
        return jnp.where(lane_row == lane, value, 0.0)

    def grams(k):
        latest = column_u[k]
        row = at_lane(6, inner(latest, latest))
        for i in range(ITERS):
            value = inner(column_u[i], latest)
            row = row + at_lane(8 + i, value)
        return row

    def exchange(k, with_column):
        message = plane_w.at[k, my_p]
        if with_column:
            for _, device in plane_peers[:16]:
                send(message, message, device, 1, plane_sem.at[k])
            for device in column_peers:
                send(message, column_w.at[k, my_z], device, 0, column_sem.at[k])
            for _, device in plane_peers[16:]:
                send(message, message, device, 1, plane_sem.at[k])
        else:
            for _, device in plane_peers:
                send(message, message, device, 1, plane_sem.at[k])
        arrived(plane_w.at[k, pl.ds(0, PLANE - 1)], plane_sem.at[k])
        sums = jnp.sum(plane_w[k, :, 3, :], axis=0, keepdims=True)
        gram[pl.ds(k, 1), :] = sums
        norm = jnp.sqrt(sums[:, 6:7])
        scaled = 1.0 / norm
        inverse[pl.ds(k, 1), :] = jnp.broadcast_to(scaled, (1, LANES))
        table = jnp.where((hes_rows == k) & (hes_lanes == k - 1), norm, hes[0:8])
        factors = []
        for i in range(ITERS):
            present = inverse[i:i + 1, 0:1]
            value = sums[:, i:i + 1] * present * scaled
            table = jnp.where((hes_rows == i) & (hes_lanes == k), value, table)
            factors.append(value * present)
        hes[0:8] = table
        hes[8:9] = jnp.where(k == 0, jnp.broadcast_to(norm, (1, LANES)), hes[8:9])
        return scaled, factors

    sent(plane_in.at[pl.ds(0, DEPTH - 1)], 0)
    sent(plane_in.at[pl.ds(0, PLANE - 1)], 1)

    def one_step(k, carry):
        partial = part_out[k]
        row = jnp.zeros((1, LANES), F32)
        for i in range(ITERS):
            row = row + at_lane(i, inner(column_u[i], partial))
        for t in range(DEPTH):
            part_out[k, t, 3:4, :] = row
        for device in column_peers:
            send(part_out.at[k, device[0]], part_in.at[k, my_z], device, 2, part_sem.at[k])
        part_in[k, my_z] = part_out[k, my_z]
        row = grams(k)
        for i in range(ITERS):
            row = row + at_lane(i, row[:, 8 + i:9 + i])
        applied = column_u[k, my_z]
        arrived(part_in.at[k, pl.ds(0, DEPTH - 1)], part_sem.at[k])
        summed = part_in[k, 0]
        for z in range(1, DEPTH):
            summed = summed + part_in[k, z]
        applied = applied + summed
        plane_w[k, my_p] = jnp.concatenate([applied[0:3], summed[3:4] + row], axis=0)
        column_w[k, my_z] = plane_w[k, my_p]
        scaled, factors = exchange(k, True)
        for s in range(PLANE):
            lanes = slice(s * LANES, (s + 1) * LANES)
            fresh = plane_w[k, s] * scaled
            for i in range(ITERS):
                fresh = fresh - factors[i] * plane_u[i, s]
            plane_u[k + 1, s] = fresh
            value = (
                coef[0, :, lanes] * fresh[0:1]
                + coef[1, :, lanes] * fresh[1:2]
                + coef[2, :, lanes] * fresh[2:3]
            )
            for piece, part in enumerate(split3(value)):
                psi[16 * piece:16 * piece + 16, lanes] = part.astype(BF16)
        arrived(column_w.at[k, pl.ds(0, DEPTH - 1)], column_sem.at[k])
        fresh = column_w[k] * scaled
        for i in range(ITERS):
            fresh = fresh - factors[i] * column_u[i]
        column_u[k + 1] = fresh
        sent(plane_w.at[0, pl.ds(0, DEPTH - 1)], 2)
        sent(plane_w.at[0, pl.ds(0, DEPTH - 1)], 0)
        sent(plane_w.at[0, pl.ds(0, PLANE - 1)], 1)
        for b in range(BLOCKS):
            both = jnp.zeros((48, WIDE), F32)
            for q in range(0, sources, DEEP):
                product = jnp.dot(
                    psi[:, q:q + DEEP], matrix[b, q:q + DEEP], preferred_element_type=F32
                )
                both = both + (product[:, 0:WIDE] + product[:, WIDE:2 * WIDE])
            to_parts(k + 1, b, both)
        return carry

    lax.fori_loop(0, ITERS - 1, one_step, 0)

    k = ITERS - 1
    for device in column_peers:
        send(part_out.at[k], part_all.at[my_z], device, 2, part_sem.at[k])
    part_all[my_z] = part_out[k]
    row = grams(k)
    arrived(part_all.at[pl.ds(0, DEPTH - 1)], part_sem.at[k])
    applied = column_u[k]
    for z in range(DEPTH):
        applied = applied + part_all[z]
    row = row + at_lane(4, inner(applied, applied))
    for i in range(ITERS):
        row = row + at_lane(i, inner(column_u[i], applied))
    column_u[k + 1] = applied
    plane_w[k, my_p] = jnp.concatenate([applied[0, 0:3], row], axis=0)
    scaled, factors = exchange(k, False)
    fresh = column_u[k + 1, my_z] * scaled
    for i in range(ITERS):
        fresh = fresh - factors[i] * column_u[i, my_z]
    column_u[k + 1, my_z] = fresh

    present = [inverse[i:i + 1, 0:1] for i in range(ITERS)]
    tall = [hes[i:i + 1, ITERS - 1:ITERS] for i in range(ITERS)]
    whole = gram[ITERS - 1:ITERS, 4:5] * present[-1] * present[-1]
    square = whole
    for i in range(ITERS):
        square = square - tall[i] * tall[i]
        for j in range(i + 1, ITERS):
            square = square + 2.0 * (tall[i] * present[i]) * (tall[j] * present[j]) * (
                gram[j:j + 1, 8 + i:9 + i]
            )
    norm = jnp.sqrt(jnp.maximum(square, whole * 1e-14))
    inverse[ITERS:ITERS + 1, :] = jnp.broadcast_to(1.0 / norm, (1, LANES))
    table = jnp.where((hes_rows == ITERS) & (hes_lanes == ITERS - 1), norm, hes[0:8])
    packed_ref[8:16] = table
    entry = [[table[i:i + 1, k:k + 1] for k in range(ITERS)] for i in range(ITERS + 1)]
    beta = hes[8:9, 0:1]
    y = least_squares(
        [[entry[i][k] for i in range(k + 1)] for k in range(ITERS)],
        [entry[k + 1][k] for k in range(ITERS)],
        beta,
    )
    solved = jnp.zeros((4, LANES), F32)
    misfit = jnp.zeros((4, LANES), F32)
    for i in range(ITERS + 1):
        basis = column_u[i, my_z] * inverse[i:i + 1, :]
        if i < ITERS:
            solved = solved + y[i] * basis
        g = beta if i == 0 else jnp.zeros_like(beta)
        for k in range(max(i - 1, 0), ITERS):
            g = g - entry[i][k] * y[k]
        misfit = misfit + g * basis
    packed_ref[0:4] = solved
    packed_ref[4:8] = misfit
    sent(part_all.at[pl.ds(0, DEPTH - 1)], 2)
    sent(plane_w.at[0, pl.ds(0, PLANE - 1)], 1)


def unpack(packed_ref, sol_ref, res_ref, hes_ref):
    sol_ref[...] = packed_ref[0:3]
    res_ref[...] = packed_ref[4:7]
    hes_ref[...] = packed_ref[8:16].T[0:ITERS, 0:ITERS + 1]


def shards(positions, areas, right_side):
    vmem = pl.BlockSpec(memory_space=pltpu.VMEM)
    sources, targets = PLANE * LANES, DEPTH * LANES
    packed = pl.pallas_call(
        kernel,
        out_shape=jax.ShapeDtypeStruct((16, LANES), F32),
        in_specs=[pl.BlockSpec(memory_space=pl.ANY)] * 3,
        out_specs=vmem,
        scratch_shapes=[
            pltpu.VMEM((PLANE, 8, LANES), F32),
            pltpu.VMEM((DEPTH, 8, LANES), F32),
            pltpu.VMEM((BLOCKS, sources, 2 * WIDE), BF16),
            pltpu.VMEM((48, sources), BF16),
            pltpu.VMEM((48, targets), BF16),
            pltpu.VMEM((3, 16, sources), F32),
            pltpu.VMEM((3, 16, targets), F32),
            pltpu.VMEM((48, sources), BF16),
            pltpu.VMEM((48, targets), F32),
            pltpu.VMEM((ITERS, PLANE, 4, LANES), F32),
            pltpu.VMEM((ITERS, DEPTH, 4, LANES), F32),
            pltpu.VMEM((ITERS, DEPTH, 4, LANES), F32),
            pltpu.VMEM((ITERS, DEPTH, 4, LANES), F32),
            pltpu.VMEM((DEPTH, DEPTH, 4, LANES), F32),
            pltpu.VMEM((ITERS + 1, PLANE, 4, LANES), F32),
            pltpu.VMEM((ITERS + 1, DEPTH, 4, LANES), F32),
            pltpu.VMEM((8, LANES), F32),
            pltpu.VMEM((16, LANES), F32),
            pltpu.VMEM((8, LANES), F32),
            pltpu.SemaphoreType.DMA((3,)),
            pltpu.SemaphoreType.DMA((3,)),
            pltpu.SemaphoreType.DMA((ITERS + 4,)),
            pltpu.SemaphoreType.DMA((ITERS + 1,)),
            pltpu.SemaphoreType.DMA((ITERS,)),
        ],
        compiler_params=pltpu.CompilerParams(
            collective_id=0, has_side_effects=True, vmem_limit_bytes=56 * 1024 * 1024
        ),
        name="arnoldi",
    )(positions, areas.reshape(1, -1), right_side)
    solved, misfit, turned = pl.pallas_call(
        unpack,
        out_shape=(
            jax.ShapeDtypeStruct((3, LANES), F32),
            jax.ShapeDtypeStruct((3, LANES), F32),
            jax.ShapeDtypeStruct((ITERS, ITERS + 1), F32),
        ),
        in_specs=[vmem],
        out_specs=(vmem,) * 3,
        name="unpack",
    )(packed)
    return solved, misfit, turned.T


def solution(mesh):
    split = Mesh(mesh.devices.reshape(DEPTH, PLANE), ("z", "p"))
    return jax.shard_map(
        shards,
        mesh=split,
        in_specs=(P(None, ("z", "p")), P(("z", "p")), P(None, ("z", "p"))),
        out_specs=(P(None, ("z", "p")), P(None, ("z", "p")), P()),
        check_vma=False,
    )
```

time: 84 us -> 76.3 us (0.908)
  Pallas kernels: 83.2 us -> 75.4 us
    pallas_call x1, Pallas kernels: 81.8 us -> 74.1 us  [shards(): pl.pallas_call(kernel, out_shape=jax.ShapeDtypeStruct((16, LANES), F32),...]
where the time goes in v3:
time: 76.3 us; the launch traced here: 76.1 us
  Pallas kernels  75.4 us (99%)
    pallas_call x1, Pallas kernels, shards(): pl.pallas_call(kernel, out_shape=jax.ShapeDtypeStruct((16, LANES), F32),...  74.1 us

profile of v3, /device:TPU:1, one launch (start us, length us, event | category | flops | bytes accessed | tf_op | source)
XLA Modules:
  0.0 76.1 jit_solution(14715485530528172010)
XLA Ops:
  0.6 74.1 %arnoldi.1.packed_ref = f32[16,128]{1,0:T(8,128)} custom-call(f32[3,128]{1,0:T(4,128)} %pos_ref.1, f32[1,128]{1,0:T(1,128)} %bitcast.2, f32[3,128]{1,0:T(4,128)} %rhs_ref.1), custom_call_target="tpu_custom_call" | custom-call | tf_op jit(solution)/shard_map/arnoldi/pallas_call | solution.py:421
  74.7 1.3 %unpack.1 = (f32[3,128]{1,0:T(4,128)}, f32[3,128]{1,0:T(4,128)}, f32[4,5]{1,0:T(4,128)}) custom-call(f32[16,128]{1,0:T(8,128)} %arnoldi.1.packed_ref), custom_call_target="tpu_custom_call" | custom-call | tf_op jit(solution)/shard_map/unpack/pallas_call | solution.py:457

commit v4 on v3

--- a/solution.py
+++ b/solution.py
@@ -12,8 +12,8 @@
 soften = 0.0025
 LANES = 128
 WIDE = 256
-CHUNK = 512
-DEEP = 1024
+CHUNK = 4096
+DEEP = 512
 DEPTH = 8
 PLANE = 32
 BLOCKS = DEPTH * LANES // WIDE
@@ -236,26 +236,38 @@
 
     lax.fori_loop(0, sources // CHUNK, factor_block, 0)
 
-    def to_parts(k, b, both):
+    lane_row = lax.broadcasted_iota(jnp.int32, (1, LANES), 1)
+    hes_rows, hes_lanes = row_iota(8), lax.broadcasted_iota(jnp.int32, (8, LANES), 1)
+
+    def at_lane(lane, value):
+        return jnp.where(lane_row == lane, value, 0.0)
+
+    def to_parts(k, b, both, dots):
         summed = both[0:16] + both[16:32] + both[32:48]
+        dots = list(dots)
         for a in range(3):
             row = jnp.sum(phi[a, :, b * WIDE:(b + 1) * WIDE] * summed, axis=0, keepdims=True)
             for c in range(WIDE // LANES):
-                part_out[k, b * (WIDE // LANES) + c, a:a + 1, :] = (
-                    row[:, c * LANES:(c + 1) * LANES]
-                )
-
+                t, piece = b * (WIDE // LANES) + c, row[:, c * LANES:(c + 1) * LANES]
+                part_out[k, t, a:a + 1, :] = piece
+                for i in range(ITERS):
+                    dots[i] = dots[i] + column_u[i, t, a:a + 1, :] * piece
+        return dots
+
+    def with_dots(k, dots):
+        row = jnp.zeros((1, LANES), F32)
+        for i in range(ITERS):
+            row = row + at_lane(i, jnp.sum(dots[i], axis=1, keepdims=True))
+        for t in range(DEPTH):
+            part_out[k, t, 3:4, :] = row
+
+    dots = [jnp.zeros((1, LANES), F32)] * ITERS
     for b in range(BLOCKS):
-        to_parts(0, b, image[:, b * WIDE:(b + 1) * WIDE])
-
-    lane_row = lax.broadcasted_iota(jnp.int32, (1, LANES), 1)
-    hes_rows, hes_lanes = row_iota(8), lax.broadcasted_iota(jnp.int32, (8, LANES), 1)
+        dots = to_parts(0, b, image[:, b * WIDE:(b + 1) * WIDE], dots)
+    with_dots(0, dots)
 
     def inner(left, right):
         return total_of(jnp.sum(left * right, axis=0)[0:3])
-
-    def at_lane(lane, value):
-        return jnp.where(lane_row == lane, value, 0.0)
 
     def grams(k):
         latest = column_u[k]
@@ -298,12 +310,6 @@
     sent(plane_in.at[pl.ds(0, PLANE - 1)], 1)
 
     def one_step(k, carry):
-        partial = part_out[k]
-        row = jnp.zeros((1, LANES), F32)
-        for i in range(ITERS):
-            row = row + at_lane(i, inner(column_u[i], partial))
-        for t in range(DEPTH):
-            part_out[k, t, 3:4, :] = row
         for device in column_peers:
             send(part_out.at[k, device[0]], part_in.at[k, my_z], device, 2, part_sem.at[k])
         part_in[k, my_z] = part_out[k, my_z]
@@ -340,6 +346,7 @@
         sent(plane_w.at[0, pl.ds(0, DEPTH - 1)], 2)
         sent(plane_w.at[0, pl.ds(0, DEPTH - 1)], 0)
         sent(plane_w.at[0, pl.ds(0, PLANE - 1)], 1)
+        dots = [jnp.zeros((1, LANES), F32)] * ITERS
         for b in range(BLOCKS):
             both = jnp.zeros((48, WIDE), F32)
             for q in range(0, sources, DEEP):
@@ -347,7 +354,8 @@
                     psi[:, q:q + DEEP], matrix[b, q:q + DEEP], preferred_element_type=F32
                 )
                 both = both + (product[:, 0:WIDE] + product[:, WIDE:2 * WIDE])
-            to_parts(k + 1, b, both)
+            dots = to_parts(k + 1, b, both, dots)
+        with_dots(k + 1, dots)
         return carry
 
     lax.fori_loop(0, ITERS - 1, one_step, 0)
@@ -420,7 +428,7 @@
     sources, targets = PLANE * LANES, DEPTH * LANES
     packed = pl.pallas_call(
         kernel,
-        out_shape=jax.ShapeDtypeStruct((16, LANES), F32),
+        out_shape=pltpu.VMEM((16, LANES), F32),
         in_specs=[pl.BlockSpec(memory_space=pl.ANY)] * 3,
         out_specs=vmem,
         scratch_shapes=[
@@ -464,7 +472,7 @@
         in_specs=[vmem],
         out_specs=(vmem,) * 3,
         name="unpack",
-    )(packed)
+    )(pltpu.with_memory_space_constraint(packed, pltpu.VMEM))
     return solved, misfit, turned.T
 
 

time: 76.3 us -> 72.5 us (0.950)
  Pallas kernels: 75.4 us -> 71.8 us
    pallas_call x1, Pallas kernels: 74.1 us -> 71.1 us  [shards(): pl.pallas_call(kernel, out_shape=pltpu.VMEM((16, LANES), F32), in_specs=[...]
where the time goes in v4:
time: 72.5 us; the launch traced here: 72.4 us
  Pallas kernels  71.8 us (99%)
    pallas_call x1, Pallas kernels, shards(): pl.pallas_call(kernel, out_shape=pltpu.VMEM((16, LANES), F32), in_specs=[...  71.1 us

profile of v4, /device:TPU:1, one launch (start us, length us, event | category | flops | bytes accessed | tf_op | source)
XLA Modules:
  0.0 72.4 jit_solution(17239352900622770243)
XLA Ops:
  0.6 71.1 %arnoldi.1.packed_ref = f32[16,128]{1,0:T(8,128)S(1)} custom-call(f32[3,128]{1,0:T(4,128)} %pos_ref.1, f32[1,128]{1,0:T(1,128)} %bitcast.2, f32[3,128]{1,0:T(4,128)} %rhs_ref.1), custom_call_target="tpu_custom_call" | custom-call | tf_op jit(solution)/shard_map/arnoldi/pallas_call | solution.py:429
  71.7 0.6 unpack.1

commit v5 on v4

--- a/solution.py
+++ b/solution.py
@@ -250,18 +250,18 @@
             for c in range(WIDE // LANES):
                 t, piece = b * (WIDE // LANES) + c, row[:, c * LANES:(c + 1) * LANES]
                 part_out[k, t, a:a + 1, :] = piece
-                for i in range(ITERS):
+                for i in range(len(dots)):
                     dots[i] = dots[i] + column_u[i, t, a:a + 1, :] * piece
         return dots
 
     def with_dots(k, dots):
         row = jnp.zeros((1, LANES), F32)
-        for i in range(ITERS):
+        for i in range(len(dots)):
             row = row + at_lane(i, jnp.sum(dots[i], axis=1, keepdims=True))
         for t in range(DEPTH):
             part_out[k, t, 3:4, :] = row
 
-    dots = [jnp.zeros((1, LANES), F32)] * ITERS
+    dots = [jnp.zeros((1, LANES), F32)]
     for b in range(BLOCKS):
         dots = to_parts(0, b, image[:, b * WIDE:(b + 1) * WIDE], dots)
     with_dots(0, dots)
@@ -271,11 +271,11 @@
 
     def grams(k):
         latest = column_u[k]
-        row = at_lane(6, inner(latest, latest))
-        for i in range(ITERS):
-            value = inner(column_u[i], latest)
-            row = row + at_lane(8 + i, value)
-        return row
+        values = [inner(column_u[i], latest) for i in range(k + 1)]
+        row = at_lane(6, values[k])
+        for i in range(k + 1):
+            row = row + at_lane(8 + i, values[i])
+        return row, values
 
     def exchange(k, with_column):
         message = plane_w.at[k, my_p]
@@ -291,31 +291,42 @@
                 send(message, message, device, 1, plane_sem.at[k])
         arrived(plane_w.at[k, pl.ds(0, PLANE - 1)], plane_sem.at[k])
         sums = jnp.sum(plane_w[k, :, 3, :], axis=0, keepdims=True)
-        gram[pl.ds(k, 1), :] = sums
+        gram[k:k + 1, :] = sums
         norm = jnp.sqrt(sums[:, 6:7])
         scaled = 1.0 / norm
-        inverse[pl.ds(k, 1), :] = jnp.broadcast_to(scaled, (1, LANES))
-        table = jnp.where((hes_rows == k) & (hes_lanes == k - 1), norm, hes[0:8])
+        inverse[k:k + 1, :] = jnp.broadcast_to(scaled, (1, LANES))
+        table = hes[0:8]
+        if k > 0:
+            table = jnp.where((hes_rows == k) & (hes_lanes == k - 1), norm, table)
         factors = []
-        for i in range(ITERS):
-            present = inverse[i:i + 1, 0:1]
+        for i in range(k + 1):
+            present = scaled if i == k else inverse[i:i + 1, 0:1]
             value = sums[:, i:i + 1] * present * scaled
             table = jnp.where((hes_rows == i) & (hes_lanes == k), value, table)
             factors.append(value * present)
         hes[0:8] = table
-        hes[8:9] = jnp.where(k == 0, jnp.broadcast_to(norm, (1, LANES)), hes[8:9])
+        if k == 0:
+            hes[8:9] = jnp.broadcast_to(norm, (1, LANES))
         return scaled, factors
 
     sent(plane_in.at[pl.ds(0, DEPTH - 1)], 0)
     sent(plane_in.at[pl.ds(0, PLANE - 1)], 1)
 
-    def one_step(k, carry):
+    def last_parts(first, slot):
+        half = pl.ds(first, DEPTH // 2)
+        for device in column_peers:
+            send(
+                part_out.at[ITERS - 1, half, 0:3], part_all.at[my_z, half, 0:3], device, 2 + slot,
+                part_sem.at[ITERS - 1 + slot],
+            )
+
+    for k in range(ITERS - 1):
         for device in column_peers:
             send(part_out.at[k, device[0]], part_in.at[k, my_z], device, 2, part_sem.at[k])
         part_in[k, my_z] = part_out[k, my_z]
-        row = grams(k)
-        for i in range(ITERS):
-            row = row + at_lane(i, row[:, 8 + i:9 + i])
+        row, values = grams(k)
+        for i in range(k + 1):
+            row = row + at_lane(i, values[i])
         applied = column_u[k, my_z]
         arrived(part_in.at[k, pl.ds(0, DEPTH - 1)], part_sem.at[k])
         summed = part_in[k, 0]
@@ -328,7 +339,7 @@
         for s in range(PLANE):
             lanes = slice(s * LANES, (s + 1) * LANES)
             fresh = plane_w[k, s] * scaled
-            for i in range(ITERS):
+            for i in range(k + 1):
                 fresh = fresh - factors[i] * plane_u[i, s]
             plane_u[k + 1, s] = fresh
             value = (
@@ -340,13 +351,14 @@
                 psi[16 * piece:16 * piece + 16, lanes] = part.astype(BF16)
         arrived(column_w.at[k, pl.ds(0, DEPTH - 1)], column_sem.at[k])
         fresh = column_w[k] * scaled
-        for i in range(ITERS):
+        for i in range(k + 1):
             fresh = fresh - factors[i] * column_u[i]
         column_u[k + 1] = fresh
         sent(plane_w.at[0, pl.ds(0, DEPTH - 1)], 2)
         sent(plane_w.at[0, pl.ds(0, DEPTH - 1)], 0)
         sent(plane_w.at[0, pl.ds(0, PLANE - 1)], 1)
-        dots = [jnp.zeros((1, LANES), F32)] * ITERS
+        final = k + 1 == ITERS - 1
+        dots = [jnp.zeros((1, LANES), F32)] * (0 if final else k + 2)
         for b in range(BLOCKS):
             both = jnp.zeros((48, WIDE), F32)
             for q in range(0, sources, DEEP):
@@ -355,17 +367,18 @@
                 )
                 both = both + (product[:, 0:WIDE] + product[:, WIDE:2 * WIDE])
             dots = to_parts(k + 1, b, both, dots)
-        with_dots(k + 1, dots)
-        return carry
-
-    lax.fori_loop(0, ITERS - 1, one_step, 0)
+            if final and b == BLOCKS // 2 - 1:
+                last_parts(0, 0)
+        if final:
+            last_parts(DEPTH // 2, 1)
+        else:
+            with_dots(k + 1, dots)
 
     k = ITERS - 1
-    for device in column_peers:
-        send(part_out.at[k], part_all.at[my_z], device, 2, part_sem.at[k])
     part_all[my_z] = part_out[k]
-    row = grams(k)
-    arrived(part_all.at[pl.ds(0, DEPTH - 1)], part_sem.at[k])
+    row, _ = grams(k)
+    for slot in range(2):
+        arrived(part_all.at[pl.ds(0, DEPTH - 1), pl.ds(0, DEPTH // 2), 0:3], part_sem.at[k + slot])
     applied = column_u[k]
     for z in range(DEPTH):
         applied = applied + part_all[z]
@@ -413,7 +426,8 @@
         misfit = misfit + g * basis
     packed_ref[0:4] = solved
     packed_ref[4:8] = misfit
-    sent(part_all.at[pl.ds(0, DEPTH - 1)], 2)
+    for slot in range(2):
+        sent(part_all.at[pl.ds(0, DEPTH - 1), pl.ds(0, DEPTH // 2), 0:3], 2 + slot)
     sent(plane_w.at[0, pl.ds(0, PLANE - 1)], 1)
 
 
@@ -452,10 +466,10 @@
             pltpu.VMEM((16, LANES), F32),
             pltpu.VMEM((8, LANES), F32),
             pltpu.SemaphoreType.DMA((3,)),
-            pltpu.SemaphoreType.DMA((3,)),
+            pltpu.SemaphoreType.DMA((4,)),
             pltpu.SemaphoreType.DMA((ITERS + 4,)),
             pltpu.SemaphoreType.DMA((ITERS + 1,)),
-            pltpu.SemaphoreType.DMA((ITERS,)),
+            pltpu.SemaphoreType.DMA((ITERS + 1,)),
         ],
         compiler_params=pltpu.CompilerParams(
             collective_id=0, has_side_effects=True, vmem_limit_bytes=56 * 1024 * 1024

time: 72.5 us -> 71 us (0.979)
  Pallas kernels: 71.8 us -> 70.3 us
    pallas_call x1, Pallas kernels: 71.1 us -> 69.6 us  [shards(): pl.pallas_call(kernel, out_shape=pltpu.VMEM((16, LANES), F32), in_specs=[...]
where the time goes in v5:
time: 71 us; the launch traced here: 70.9 us
  Pallas kernels  70.3 us (99%)
    pallas_call x1, Pallas kernels, shards(): pl.pallas_call(kernel, out_shape=pltpu.VMEM((16, LANES), F32), in_specs=[...  69.6 us

profile of v5, /device:TPU:1, one launch (start us, length us, event | category | flops | bytes accessed | tf_op | source)
XLA Modules:
  0.0 70.9 jit_solution(6754120303890099338)
XLA Ops:
  0.6 69.6 %arnoldi.1.packed_ref = f32[16,128]{1,0:T(8,128)S(1)} custom-call(f32[3,128]{1,0:T(4,128)} %pos_ref.1, f32[1,128]{1,0:T(1,128)} %bitcast.2, f32[3,128]{1,0:T(4,128)} %rhs_ref.1), custom_call_target="tpu_custom_call" | custom-call | tf_op jit(solution)/shard_map/arnoldi/pallas_call | solution.py:443
  70.3 0.6 unpack.1

commit v6 on v5

--- a/solution.py
+++ b/solution.py
@@ -12,7 +12,7 @@
 soften = 0.0025
 LANES = 128
 WIDE = 256
-CHUNK = 4096
+CHUNK = 512
 DEEP = 512
 DEPTH = 8
 PLANE = 32
@@ -67,7 +67,7 @@
 
 def kernel(
     pos_ref, area_ref, rhs_ref, packed_ref,
-    plane_in, column_in, matrix, sf, tf, coef, phi, psi, image,
+    plane_in, column_in, matrix, sf, tf, coef, phi, psi,
     plane_w, column_w, part_out, part_in, part_all, plane_u, column_u, gram, hes, inverse,
     load_sem, send_sem, plane_sem, column_sem, part_sem,
 ):
@@ -175,7 +175,7 @@
             one_source_block(first + s)
             return carry
 
-        lax.fori_loop(0, 8, body, 0)
+        lax.fori_loop(0, 8, body, 0, unroll=turn == 2)
 
     source_rows(0, 7)
     source_rows(1, 8)
@@ -213,29 +213,6 @@
 
     source_rows(2, 8)
 
-    image[...] = jnp.zeros_like(image)
-
-    def factor_block(s, carry):
-        rows = pl.ds(pl.multiple_of(s * CHUNK, CHUNK), CHUNK)
-        left = psi[:, rows]
-        for b in range(BLOCKS):
-            square = lax.dot_general(
-                sf[:, rows], tf[:, b * WIDE:(b + 1) * WIDE], (((0,), (0,)), ((), ())),
-                preferred_element_type=F32,
-            )
-            root = lax.rsqrt(square)
-            factor = root * root * root
-            high = factor.astype(BF16)
-            low = (factor - high.astype(F32)).astype(BF16)
-            matrix[b, rows, 0:WIDE] = high
-            matrix[b, rows, WIDE:2 * WIDE] = low
-            image[:, b * WIDE:(b + 1) * WIDE] += jnp.dot(
-                left, high, preferred_element_type=F32
-            ) + jnp.dot(left, low, preferred_element_type=F32)
-        return carry
-
-    lax.fori_loop(0, sources // CHUNK, factor_block, 0)
-
     lane_row = lax.broadcasted_iota(jnp.int32, (1, LANES), 1)
     hes_rows, hes_lanes = row_iota(8), lax.broadcasted_iota(jnp.int32, (8, LANES), 1)
 
@@ -263,7 +240,24 @@
 
     dots = [jnp.zeros((1, LANES), F32)]
     for b in range(BLOCKS):
-        dots = to_parts(0, b, image[:, b * WIDE:(b + 1) * WIDE], dots)
+        both = jnp.zeros((48, WIDE), F32)
+        for q in range(0, sources, CHUNK):
+            square = lax.dot_general(
+                sf[:, q:q + CHUNK], tf[:, b * WIDE:(b + 1) * WIDE], (((0,), (0,)), ((), ())),
+                preferred_element_type=F32,
+            )
+            root = lax.rsqrt(square)
+            factor = root * root * root
+            high = factor.astype(BF16)
+            low = (factor - high.astype(F32)).astype(BF16)
+            matrix[b, q:q + CHUNK, 0:WIDE] = high
+            matrix[b, q:q + CHUNK, WIDE:2 * WIDE] = low
+            left = psi[:, q:q + CHUNK]
+            both = both + (
+                jnp.dot(left, high, preferred_element_type=F32)
+                + jnp.dot(left, low, preferred_element_type=F32)
+            )
+        dots = to_parts(0, b, both, dots)
     with_dots(0, dots)
 
     def inner(left, right):
@@ -278,7 +272,8 @@
         return row, values
 
     def exchange(k, with_column):
-        message = plane_w.at[k, my_p]
+        whole = slice(0, 4) if with_column else slice(3, 4)
+        message = plane_w.at[k, my_p, whole]
         if with_column:
             for _, device in plane_peers[:16]:
                 send(message, message, device, 1, plane_sem.at[k])
@@ -289,7 +284,7 @@
         else:
             for _, device in plane_peers:
                 send(message, message, device, 1, plane_sem.at[k])
-        arrived(plane_w.at[k, pl.ds(0, PLANE - 1)], plane_sem.at[k])
+        arrived(plane_w.at[k, pl.ds(0, PLANE - 1), whole], plane_sem.at[k])
         sums = jnp.sum(plane_w[k, :, 3, :], axis=0, keepdims=True)
         gram[k:k + 1, :] = sums
         norm = jnp.sqrt(sums[:, 6:7])
@@ -428,7 +423,7 @@
     packed_ref[4:8] = misfit
     for slot in range(2):
         sent(part_all.at[pl.ds(0, DEPTH - 1), pl.ds(0, DEPTH // 2), 0:3], 2 + slot)
-    sent(plane_w.at[0, pl.ds(0, PLANE - 1)], 1)
+    sent(plane_w.at[0, pl.ds(0, PLANE - 1), 3:4], 1)
 
 
 def unpack(packed_ref, sol_ref, res_ref, hes_ref):
@@ -454,7 +449,6 @@
             pltpu.VMEM((3, 16, sources), F32),
             pltpu.VMEM((3, 16, targets), F32),
             pltpu.VMEM((48, sources), BF16),
-            pltpu.VMEM((48, targets), F32),
             pltpu.VMEM((ITERS, PLANE, 4, LANES), F32),
             pltpu.VMEM((ITERS, DEPTH, 4, LANES), F32),
             pltpu.VMEM((ITERS, DEPTH, 4, LANES), F32),

time: 71 us -> 70.1 us (0.987)
  Pallas kernels: 70.3 us -> 69.4 us
    pallas_call x1, Pallas kernels: 69.6 us -> 68.8 us  [shards(): pl.pallas_call(kernel, out_shape=pltpu.VMEM((16, LANES), F32), in_specs=[...]
where the time goes in v6:
time: 70.1 us; the launch traced here: 70 us
  Pallas kernels  69.4 us (99%)
    pallas_call x1, Pallas kernels, shards(): pl.pallas_call(kernel, out_shape=pltpu.VMEM((16, LANES), F32), in_specs=[...  68.8 us

profile of v6, /device:TPU:1, one launch (start us, length us, event | category | flops | bytes accessed | tf_op | source)
XLA Modules:
  0.0 70.0 jit_solution(12662651902212090903)
XLA Ops:
  0.6 68.8 %arnoldi.1.packed_ref = f32[16,128]{1,0:T(8,128)S(1)} custom-call(f32[3,128]{1,0:T(4,128)} %pos_ref.1, f32[1,128]{1,0:T(1,128)} %bitcast.2, f32[3,128]{1,0:T(4,128)} %rhs_ref.1), custom_call_target="tpu_custom_call" | custom-call | tf_op jit(solution)/shard_map/arnoldi/pallas_call | solution.py:438
  69.4 0.6 unpack.1

commit v7 on v6

--- a/solution.py
+++ b/solution.py
@@ -98,7 +98,8 @@
     ]
     for load in loads:
         load.start()
-    plane_in[my_p, 7:8, :] = jnp.zeros((1, LANES), F32)
+    plane_in[:, 7:8, :] = jnp.zeros((PLANE, 1, LANES), F32)
+    column_in[:, 7:8, :] = jnp.zeros((DEPTH, 1, LANES), F32)
     hes[...] = jnp.zeros_like(hes)
     inverse[...] = jnp.zeros_like(inverse)
     plane_u[...] = jnp.zeros_like(plane_u)
@@ -126,10 +127,13 @@
             device_id=(my_z, my_p), device_id_type=MESH,
         ).wait_send()
 
+    used = own.at[0:7]
+    for turn, device in plane_peers[:8]:
+        send(used, used, device, 1, plane_sem.at[ITERS + (4 - turn) % 4])
     for device in column_peers:
-        send(own, column_in.at[my_z], device, 0, column_sem.at[ITERS])
-    for turn, device in plane_peers:
-        send(own, own, device, 1, plane_sem.at[ITERS + (4 - turn) % 4])
+        send(used, column_in.at[my_z, 0:7], device, 0, column_sem.at[ITERS])
+    for turn, device in plane_peers[8:]:
+        send(used, used, device, 1, plane_sem.at[ITERS + (4 - turn) % 4])
     column_in[my_z] = plane_in[my_p]
 
     rows8, rows16 = row_iota(8), row_iota(16)
@@ -148,6 +152,7 @@
         sf[0:16, lanes] = jnp.concatenate([m1, m2], axis=0).astype(BF16)
         sf[16:32, lanes] = jnp.concatenate([m1, m3], axis=0).astype(BF16)
         sf[32:48, lanes] = jnp.concatenate([m1, m2], axis=0).astype(BF16)
+        sf[48:64, lanes] = jnp.concatenate([m2, m3], axis=0).astype(BF16)
         chosen = jnp.zeros((16, LANES), F32)
         for b in range(3):
             mine = ((rows16 >= 3 + 3 * b) & (rows16 < 6 + 3 * b)) | (rows16 == 12 + b)
@@ -168,7 +173,7 @@
         plane_u[0, s] = block[4:8]
 
     def source_rows(turn, count):
-        arrived(plane_in.at[pl.ds(0, count)], plane_sem.at[ITERS + turn])
+        arrived(plane_in.at[pl.ds(0, count), 0:7], plane_sem.at[ITERS + turn])
         first = ((my_y + turn) % 4) * 8
 
         def body(s, carry):
@@ -181,7 +186,7 @@
     source_rows(1, 8)
     source_rows(3, 8)
 
-    arrived(column_in.at[pl.ds(0, DEPTH - 1)], column_sem.at[ITERS])
+    arrived(column_in.at[pl.ds(0, DEPTH - 1), 0:7], column_sem.at[ITERS])
     for t in range(DEPTH):
         block = column_in[t]
         lanes = pl.ds(t * LANES, LANES)
@@ -195,6 +200,7 @@
         tf[0:16, lanes] = jnp.concatenate([t1, t1], axis=0).astype(BF16)
         tf[16:32, lanes] = jnp.concatenate([t2, t1], axis=0).astype(BF16)
         tf[32:48, lanes] = jnp.concatenate([t3, t2], axis=0).astype(BF16)
+        tf[48:64, lanes] = jnp.concatenate([t3, t2], axis=0).astype(BF16)
         for a in range(3):
             value = jnp.zeros((16, LANES), F32)
             for b in range(3):
@@ -304,8 +310,8 @@
             hes[8:9] = jnp.broadcast_to(norm, (1, LANES))
         return scaled, factors
 
-    sent(plane_in.at[pl.ds(0, DEPTH - 1)], 0)
-    sent(plane_in.at[pl.ds(0, PLANE - 1)], 1)
+    sent(plane_in.at[pl.ds(0, DEPTH - 1), 0:7], 0)
+    sent(plane_in.at[pl.ds(0, PLANE - 1), 0:7], 1)
 
     def last_parts(first, slot):
         half = pl.ds(first, DEPTH // 2)
@@ -444,8 +450,8 @@
             pltpu.VMEM((PLANE, 8, LANES), F32),
             pltpu.VMEM((DEPTH, 8, LANES), F32),
             pltpu.VMEM((BLOCKS, sources, 2 * WIDE), BF16),
-            pltpu.VMEM((48, sources), BF16),
-            pltpu.VMEM((48, targets), BF16),
+            pltpu.VMEM((64, sources), BF16),
+            pltpu.VMEM((64, targets), BF16),
             pltpu.VMEM((3, 16, sources), F32),
             pltpu.VMEM((3, 16, targets), F32),
             pltpu.VMEM((48, sources), BF16),

time: 70.1 us -> 70 us (level)
  no operation moved by 1% of the time
where the time goes in v7:
time: 70 us; the launch traced here: 69.9 us
  Pallas kernels  69.3 us (99%)
    pallas_call x1, Pallas kernels, shards(): pl.pallas_call(kernel, out_shape=pltpu.VMEM((16, LANES), F32), in_specs=[...  68.7 us

profile of v7, /device:TPU:1, one launch (start us, length us, event | category | flops | bytes accessed | tf_op | source)
XLA Modules:
  0.0 69.9 jit_solution(1664388741459878342)
XLA Ops:
  0.6 68.7 %arnoldi.1.packed_ref = f32[16,128]{1,0:T(8,128)S(1)} custom-call(f32[3,128]{1,0:T(4,128)} %pos_ref.1, f32[1,128]{1,0:T(1,128)} %bitcast.2, f32[3,128]{1,0:T(4,128)} %rhs_ref.1), custom_call_target="tpu_custom_call" | custom-call | tf_op jit(solution)/shard_map/arnoldi/pallas_call | solution.py:444
  69.3 0.6 unpack.1

commit v8 on v7

--- a/solution.py
+++ b/solution.py
@@ -88,8 +88,6 @@
     column_peers = [((my_z + d) % DEPTH, my_p) for d in (4, 3, 5, 2, 6, 1, 7)]
 
     barrier = pltpu.get_barrier_semaphore()
-    for device in column_peers + [peer for _, peer in plane_peers]:
-        pl.semaphore_signal(barrier, inc=1, device_id=device, device_id_type=MESH)
     own = plane_in.at[my_p]
     loads = [
         pltpu.make_async_copy(pos_ref, own.at[0:3], load_sem.at[0]),
@@ -98,13 +96,8 @@
     ]
     for load in loads:
         load.start()
-    plane_in[:, 7:8, :] = jnp.zeros((PLANE, 1, LANES), F32)
-    column_in[:, 7:8, :] = jnp.zeros((DEPTH, 1, LANES), F32)
-    hes[...] = jnp.zeros_like(hes)
-    inverse[...] = jnp.zeros_like(inverse)
-    plane_u[...] = jnp.zeros_like(plane_u)
-    column_u[...] = jnp.zeros_like(column_u)
-    part_out[...] = jnp.zeros_like(part_out)
+    for device in column_peers + [peer for _, peer in plane_peers]:
+        pl.semaphore_signal(barrier, inc=1, device_id=device, device_id_type=MESH)
     for load in loads:
         load.wait()
     pl.semaphore_wait(barrier, PLANE - 1 + DEPTH - 1)
@@ -134,7 +127,11 @@
         send(used, column_in.at[my_z, 0:7], device, 0, column_sem.at[ITERS])
     for turn, device in plane_peers[8:]:
         send(used, used, device, 1, plane_sem.at[ITERS + (4 - turn) % 4])
+    plane_in[:, 7:8, :] = jnp.zeros((PLANE, 1, LANES), F32)
+    column_in[:, 7:8, :] = jnp.zeros((DEPTH, 1, LANES), F32)
     column_in[my_z] = plane_in[my_p]
+    hes[...] = jnp.zeros_like(hes)
+    part_out[ITERS - 1] = jnp.zeros((DEPTH, 4, LANES), F32)
 
     rows8, rows16 = row_iota(8), row_iota(16)
     scale = float(PLANE * DEPTH * LANES) ** (-0.5)

time: 70 us -> 70 us (level)
  no operation moved by 1% of the time
where the time goes in v8:
time: 70 us; the launch traced here: 69.9 us
  Pallas kernels  69.3 us (99%)
    pallas_call x1, Pallas kernels, shards(): pl.pallas_call(kernel, out_shape=pltpu.VMEM((16, LANES), F32), in_specs=[...  68.6 us

profile of v8, /device:TPU:1, one launch (start us, length us, event | category | flops | bytes accessed | tf_op | source)
XLA Modules:
  0.0 69.9 jit_solution(9086920678231469997)
XLA Ops:
  0.6 68.6 %arnoldi.1.packed_ref = f32[16,128]{1,0:T(8,128)S(1)} custom-call(f32[3,128]{1,0:T(4,128)} %pos_ref.1, f32[1,128]{1,0:T(1,128)} %bitcast.2, f32[3,128]{1,0:T(4,128)} %rhs_ref.1), custom_call_target="tpu_custom_call" | custom-call | tf_op jit(solution)/shard_map/arnoldi/pallas_call | solution.py:441
  69.3 0.6 unpack.1

commit v9 on v8

--- a/solution.py
+++ b/solution.py
@@ -242,12 +242,13 @@
             part_out[k, t, 3:4, :] = row
 
     dots = [jnp.zeros((1, LANES), F32)]
-    for b in range(BLOCKS):
-        both = jnp.zeros((48, WIDE), F32)
-        for q in range(0, sources, CHUNK):
-            square = lax.dot_general(
-                sf[:, q:q + CHUNK], tf[:, b * WIDE:(b + 1) * WIDE], (((0,), (0,)), ((), ())),
-                preferred_element_type=F32,
+    boths = [jnp.zeros((48, WIDE), F32)] * BLOCKS
+    for q in range(0, sources, CHUNK):
+        left = psi[:, q:q + CHUNK]
+        right = sf[:, q:q + CHUNK].T
+        for b in range(BLOCKS):
+            square = jnp.dot(
+                right, tf[:, b * WIDE:(b + 1) * WIDE], preferred_element_type=F32
             )
             root = lax.rsqrt(square)
             factor = root * root * root
@@ -255,12 +256,12 @@
             low = (factor - high.astype(F32)).astype(BF16)
             matrix[b, q:q + CHUNK, 0:WIDE] = high
             matrix[b, q:q + CHUNK, WIDE:2 * WIDE] = low
-            left = psi[:, q:q + CHUNK]
-            both = both + (
+            boths[b] = boths[b] + (
                 jnp.dot(left, high, preferred_element_type=F32)
                 + jnp.dot(left, low, preferred_element_type=F32)
             )
-        dots = to_parts(0, b, both, dots)
+    for b in range(BLOCKS):
+        dots = to_parts(0, b, boths[b], dots)
     with_dots(0, dots)
 
     def inner(left, right):

time: 70 us -> 70 us (level)
  no operation moved by 1% of the time
where the time goes in v9:
time: 70 us; the launch traced here: 69.9 us
  Pallas kernels  69.3 us (99%)
    pallas_call x1, Pallas kernels, shards(): pl.pallas_call(kernel, out_shape=pltpu.VMEM((16, LANES), F32), in_specs=[...  68.7 us

profile of v9, /device:TPU:1, one launch (start us, length us, event | category | flops | bytes accessed | tf_op | source)
XLA Modules:
  0.0 69.9 jit_solution(3717122089627274437)
XLA Ops:
  0.6 68.7 %arnoldi.1.packed_ref = f32[16,128]{1,0:T(8,128)S(1)} custom-call(f32[3,128]{1,0:T(4,128)} %pos_ref.1, f32[1,128]{1,0:T(1,128)} %bitcast.2, f32[3,128]{1,0:T(4,128)} %rhs_ref.1), custom_call_target="tpu_custom_call" | custom-call | tf_op jit(solution)/shard_map/arnoldi/pallas_call | solution.py:442
  69.3 0.6 unpack.1

commit v10 on v8

--- a/solution.py
+++ b/solution.py
@@ -311,7 +311,7 @@
     sent(plane_in.at[pl.ds(0, PLANE - 1), 0:7], 1)
 
     def last_parts(first, slot):
-        half = pl.ds(first, DEPTH // 2)
+        half = pl.ds(first, DEPTH // BLOCKS)
         for device in column_peers:
             send(
                 part_out.at[ITERS - 1, half, 0:3], part_all.at[my_z, half, 0:3], device, 2 + slot,
@@ -365,18 +365,16 @@
                 )
                 both = both + (product[:, 0:WIDE] + product[:, WIDE:2 * WIDE])
             dots = to_parts(k + 1, b, both, dots)
-            if final and b == BLOCKS // 2 - 1:
-                last_parts(0, 0)
-        if final:
-            last_parts(DEPTH // 2, 1)
-        else:
+            if final:
+                last_parts(b * (DEPTH // BLOCKS), b)
+        if not final:
             with_dots(k + 1, dots)
 
     k = ITERS - 1
     part_all[my_z] = part_out[k]
     row, _ = grams(k)
-    for slot in range(2):
-        arrived(part_all.at[pl.ds(0, DEPTH - 1), pl.ds(0, DEPTH // 2), 0:3], part_sem.at[k + slot])
+    for slot in range(BLOCKS):
+        arrived(part_all.at[pl.ds(0, DEPTH - 1), pl.ds(0, DEPTH // BLOCKS), 0:3], part_sem.at[k + slot])
     applied = column_u[k]
     for z in range(DEPTH):
         applied = applied + part_all[z]
@@ -424,8 +422,8 @@
         misfit = misfit + g * basis
     packed_ref[0:4] = solved
     packed_ref[4:8] = misfit
-    for slot in range(2):
-        sent(part_all.at[pl.ds(0, DEPTH - 1), pl.ds(0, DEPTH // 2), 0:3], 2 + slot)
+    for slot in range(BLOCKS):
+        sent(part_all.at[pl.ds(0, DEPTH - 1), pl.ds(0, DEPTH // BLOCKS), 0:3], 2 + slot)
     sent(plane_w.at[0, pl.ds(0, PLANE - 1), 3:4], 1)
 
 
@@ -463,10 +461,10 @@
             pltpu.VMEM((16, LANES), F32),
             pltpu.VMEM((8, LANES), F32),
             pltpu.SemaphoreType.DMA((3,)),
-            pltpu.SemaphoreType.DMA((4,)),
+            pltpu.SemaphoreType.DMA((2 + BLOCKS,)),
             pltpu.SemaphoreType.DMA((ITERS + 4,)),
             pltpu.SemaphoreType.DMA((ITERS + 1,)),
-            pltpu.SemaphoreType.DMA((ITERS + 1,)),
+            pltpu.SemaphoreType.DMA((ITERS - 1 + BLOCKS,)),
         ],
         compiler_params=pltpu.CompilerParams(
             collective_id=0, has_side_effects=True, vmem_limit_bytes=56 * 1024 * 1024

time: 70 us -> 72 us (1.029)
  Pallas kernels: 69.3 us -> 71.3 us
    pallas_call x1, Pallas kernels: 68.6 us -> 70.6 us  [shards(): pl.pallas_call(kernel, out_shape=pltpu.VMEM((16, LANES), F32), in_specs=[...]
where the time goes in v10:
time: 72 us; the launch traced here: 71.9 us
  Pallas kernels  71.3 us (99%)
    pallas_call x1, Pallas kernels, shards(): pl.pallas_call(kernel, out_shape=pltpu.VMEM((16, LANES), F32), in_specs=[...  70.6 us

profile of v10, /device:TPU:1, one launch (start us, length us, event | category | flops | bytes accessed | tf_op | source)
XLA Modules:
  0.0 71.9 jit_solution(11600663178212263591)
XLA Ops:
  0.6 70.6 %arnoldi.1.packed_ref = f32[16,128]{1,0:T(8,128)S(1)} custom-call(f32[3,128]{1,0:T(4,128)} %pos_ref.1, f32[1,128]{1,0:T(1,128)} %bitcast.2, f32[3,128]{1,0:T(4,128)} %rhs_ref.1), custom_call_target="tpu_custom_call" | custom-call | tf_op jit(solution)/shard_map/arnoldi/pallas_call | solution.py:439
  71.3 0.6 unpack.1
